TPU v7x, 512 devices: a 8x2x16 block of a 8x8x16 slice. The times are simulated.
512 devices in a mesh: grp: 2 (over y), sp: 16 (over z), sub: 8 (over x), rep: 2 (over core).
Axes of the slice: x: 8, y: 2, z: 16, core: 2. Of those that a mesh axis runs over, the one named last changes fastest.
The devices are a block of a 8x8x16 slice.
Arguments:
- field: float32 [512, 32, 32, 128], P(('grp', 'sp', 'rep'), 'sub'), parts along dimension 0, may hold values from -40 to 40, as said below
- mix_weight: float32 [256, 256], replicated, may hold values from -0.375 to 0.375
- factor_x: float32 [256, 32], replicated, may hold values from -6 to 6
- factor_y: float32 [256, 32], replicated, may hold values from -6 to 6
- factor_z: float32 [256, 32], replicated, may hold values from -6 to 6
- norm_gain: float32 [256], replicated, may hold values from 0.5 to 1.5
- norm_bias: float32 [256], replicated, may hold values from -3 to 3
- w_in: float32 [256, 256], replicated, may hold values from -0.375 to 0.375
- b_in: float32 [256], replicated, may hold values from -3 to 3
- w_out: float32 [256, 256], replicated, may hold values from -0.375 to 0.375
- b_out: float32 [256], replicated, may hold values from -3 to 3
Outputs:
- block_out: float32 [512, 32, 32, 128], P('grp', 'sub', ('sp', 'rep')), parts along dimension 0
There are 2 independent parts, one for each index of `grp`. A program takes and returns all parts, laid end to end along the dimension named above; an argument that names none is the same for every part. Nothing has to cross between parts.
Inputs may be any that keep to these rules, and one draw needn't show every extreme that they name: `field`: real values of order one in each channel, with scales that differ between channels.
All inputs are finite; a program needn't handle non-finite values.
Results may differ from a plain program's by a relative error of at most 0.000078.
Values sent between devices are 32-bit elements; how exact they have to be, the bound alone decides.
A program may use at most 64 MiB of HBM per device.

v0:
```python
import math

import jax
import jax.numpy as jnp
from jax import lax
from jax.sharding import PartitionSpec as P

C = 256
KX = 32
KY = 32
KZ = 32
GROUPS = 32
NX = 32
NY = 32
NZ = 128


def one_axis_at_a_time(shard, axes):
    for axis in axes:
        shard = lax.psum(shard, axis)
    return shard


def contract(formula, left, right):
    return jnp.einsum(formula, left, right, precision=lax.Precision.HIGHEST)


def tables(length, kept_count):
    indices = jnp.arange(kept_count, dtype=jnp.int32)
    kept_freq = jnp.where(indices < kept_count // 2, indices, length - kept_count + indices)
    positions = jnp.arange(length, dtype=jnp.int32)
    phases = kept_freq[:, None] * positions[None, :] % length
    angles = 2.0 * math.pi / length * phases.astype(jnp.float32)
    return (jnp.cos(angles), jnp.sin(angles))


def transform(planes, cosine, sine, formula):
    real_part = contract(formula, planes[0], cosine) + contract(formula, planes[1], sine)
    imag_part = contract(formula, planes[1], cosine) - contract(formula, planes[0], sine)
    return jnp.stack([real_part, imag_part])


def forward_z(values, cos_z, sin_z):
    return jnp.stack(
        [
            contract("cxyz,kz->ckxy", values, cos_z / NZ),
            -contract("cxyz,kz->ckxy", values, sin_z / NZ),
        ]
    )


def local(
    field, mix_weight, factor_x, factor_y, factor_z, norm_gain, norm_bias, w_in, b_in, w_out, b_out
):
    cos_x, sin_x = tables(NX, KX)
    cos_y, sin_y = tables(NY, KY)
    cos_z, sin_z = tables(NZ, KZ)
    wide_count = lax.axis_size(("sp", "rep"))
    narrow_count = lax.axis_size("sub")
    x_local = NX // narrow_count
    y_local = NY // wide_count
    ky_local = KY // narrow_count
    kz_local = KZ // wide_count
    x_cos = (cos_x / NX).reshape(KX, narrow_count, x_local)
    x_sin = (sin_x / NX).reshape(KX, narrow_count, x_local)
    spatial = lax.all_to_all(field, ("sp", "rep"), split_axis=2, concat_axis=0, tiled=True)
    planes = forward_z(spatial, cos_z, sin_z)
    planes = planes.reshape(2, C, -1)
    planes = lax.all_to_all(planes, ("sp", "rep"), split_axis=2, concat_axis=2, tiled=True)
    planes = planes.reshape(2, C, wide_count, kz_local, x_local, y_local)
    y_cos = (cos_y / NY).reshape(KY, wide_count, y_local)
    y_sin = (sin_y / NY).reshape(KY, wide_count, y_local)
    planes = transform(planes, y_cos, y_sin, "cskxy,jsy->cjkx")
    planes = planes.reshape(2, C, -1)
    planes = lax.all_to_all(planes, "sub", split_axis=2, concat_axis=2, tiled=True)
    planes = planes.reshape(2, C, narrow_count, ky_local, kz_local, x_local)
    spectra = transform(planes, x_cos, x_sin, "csjkx,isx->ckji")
    spectra = spectra.reshape(2, C, -1)
    factor_ky = lax.dynamic_slice_in_dim(factor_y, lax.axis_index("sub") * ky_local, ky_local, 1)
    factor_kz = lax.dynamic_slice_in_dim(
        factor_z, lax.axis_index(("sp", "rep")) * kz_local, kz_local, 1
    )
    weighting = (
        factor_kz[:, :, None, None] * factor_ky[:, None, :, None] * factor_x[:, None, None, :]
    )
    weighting = weighting.reshape(C, -1)
    mixed_modes = contract("oc,rcm->rom", mix_weight, spectra * weighting[None])
    mixed_modes = mixed_modes.reshape(2, C, kz_local, ky_local, KX)
    returned = transform(mixed_modes, cos_x, -sin_x, "ckji,ix->cxkj")
    returned = returned.reshape(2, C, -1)
    returned = lax.all_to_all(returned, "sub", split_axis=2, concat_axis=2, tiled=True)
    returned = returned.reshape(2, C, narrow_count, x_local, kz_local, ky_local)
    back_cos = cos_y.reshape(narrow_count, ky_local, NY)
    back_sin = (-sin_y).reshape(narrow_count, ky_local, NY)
    returned = transform(returned, back_cos, back_sin, "csxkj,sjy->cyxk")
    returned = returned.reshape(2, C, -1)
    returned = lax.all_to_all(returned, ("sp", "rep"), split_axis=2, concat_axis=2, tiled=True)
    returned = returned.reshape(2, C, wide_count, y_local, x_local, kz_local)
    z_cos = cos_z.reshape(wide_count, kz_local, NZ)
    z_sin = sin_z.reshape(wide_count, kz_local, NZ)
    spectral = contract("csyxk,skz->cxyz", returned[0], z_cos) - contract(
        "csyxk,skz->cxyz", returned[1], z_sin
    )
    summed = spatial + spectral
    columns = summed.reshape(C, -1)
    cells_group = C // GROUPS * NX * NY * NZ
    grouped = columns.reshape(GROUPS, -1)
    first_sum, second_sum = (
        one_axis_at_a_time(jnp.sum(grouped, axis=1), ("sp", "sub", "rep")),
        one_axis_at_a_time(jnp.sum(grouped * grouped, axis=1), ("sp", "sub", "rep")),
    )
    group_mean = first_sum / cells_group
    group_var = second_sum / cells_group - group_mean * group_mean
    inv_scale = jnp.repeat(lax.rsqrt(group_var + 1e-05), C // GROUPS) * norm_gain
    mean_chan = jnp.repeat(group_mean, C // GROUPS)
    normed = (columns - mean_chan[:, None]) * inv_scale[:, None] + norm_bias[:, None]
    hidden = jax.nn.gelu(jnp.dot(w_in, normed, precision=lax.Precision.HIGHEST) + b_in[:, None])
    result = columns + jnp.dot(w_out, hidden, precision=lax.Precision.HIGHEST) + b_out[:, None]
    return result.reshape(summed.shape)


def solution(mesh):
    placed = (
        P(("grp", "sp", "rep"), "sub", None, None),
        P(),
        P(),
        P(),
        P(),
        P(),
        P(),
        P(),
        P(),
        P(),
        P(),
    )
    return jax.shard_map(
        local,
        mesh=mesh,
        in_specs=placed,
        out_specs=P("grp", "sub", ("sp", "rep"), None),
        check_vma=False,
    )
```

profile of v0, /device:TPU:80, one launch (start us, length us, event | category | flops | bytes accessed | tf_op | source)
XLA Modules:
  0.0 234.0 jit_solution(11209274981978401408)
XLA Ops:
  0.0 2.2 copy.48
  2.2 44.4 %all-to-all-start = ((f32[8,4,32,128]{3,0,1,2:T(8,128)}), f32[8,4,32,128]{3,0,1,2:T(8,128)S(1)}, u32[]{:S(2)}, u32[]{:S(2)}) async-start(f32[8,4,32,128]{3,0,1,2:T(8,128)} %copy.48), calls=%async_computation | async-start | bytes 1048576 | tf_op jit(solution)/shard_map/all_to_all | solution.py:66
  46.7 33.1 %all-to-all-done = f32[8,4,32,128]{3,0,1,2:T(8,128)S(1)} async-done(((f32[8,4,32,128]{3,0,1,2:T(8,128)}), f32[8,4,32,128]{3,0,1,2:T(8,128)S(1)}, u32[]{:S(2)}, u32[]{:S(2)}) %all-to-all-start) | async-done | bytes 524320 | tf_op jit(solution)/shard_map/all_to_all | solution.py:66
  79.7 0.7 convolution_bitcast_fusion.2
  80.6 0.7 fusion.5
  81.5 0.9 pad_maximum_fusion
  82.4 4.8 %all-to-all-start.1 = ((f32[2,256,128]{1,0,2:T(2,128)}), f32[2,256,128]{1,0,2:T(2,128)S(1)}, u32[]{:S(2)}, u32[]{:S(2)}) async-start(f32[2,256,128]{1,0,2:T(2,128)} %pad_maximum_fusion), calls=%async_computation.1 | async-start | bytes 524288 | tf_op jit(solution)/shard_map/all_to_all | solution.py:69
  87.2 21.9 %all-to-all-done.1 = f32[2,256,128]{1,0,2:T(2,128)S(1)} async-done(((f32[2,256,128]{1,0,2:T(2,128)}), f32[2,256,128]{1,0,2:T(2,128)S(1)}, u32[]{:S(2)}, u32[]{:S(2)}) %all-to-all-start.1) | async-done | bytes 262176 | tf_op jit(solution)/shard_map/all_to_all | solution.py:69
  109.2 0.7 slice_reduce_fusion.7
  109.9 0.4 fusion.44
  110.3 0.4 fusion.48
  110.7 0.4 fusion.8
  111.1 0.4 fusion.9
  111.8 0.9 pad_maximum_fusion.1
  112.8 7.4 %all-to-all-start.2 = ((f32[2,256,128]{1,0,2:T(2,128)}), f32[2,256,128]{1,0,2:T(2,128)S(1)}, u32[]{:S(2)}, u32[]{:S(2)}) async-start(f32[2,256,128]{1,0,2:T(2,128)} %pad_maximum_fusion.1), calls=%async_computation.2 | async-start | bytes 524288 | tf_op jit(solution)/shard_map/all_to_all | solution.py:75
  120.2 0.7 constant_dynamic-slice_fusion
  120.9 0.7 dynamic-slice_multiply_fusion
  121.6 9.6 %all-to-all-done.2 = f32[2,256,128]{1,0,2:T(2,128)S(1)} async-done(((f32[2,256,128]{1,0,2:T(2,128)}), f32[2,256,128]{1,0,2:T(2,128)S(1)}, u32[]{:S(2)}, u32[]{:S(2)}) %all-to-all-start.2) | async-done | bytes 262176 | tf_op jit(solution)/shard_map/all_to_all | solution.py:75
  131.2 0.7 slice_reduce_fusion.4
  132.0 0.5 convolution_bitcast_fusion.7
  132.5 0.5 convolution_bitcast_fusion.9
  132.9 0.5 fusion.11
  133.4 0.5 fusion.10
  133.9 0.5 copy-done.1
  134.3 0.4 convolution_bitcast_fusion.1
  134.8 0.3 fusion.81
  136.7 13.0 %all_to_all.38 = f32[2,256,128]{1,0,2:T(2,128)S(1)} all-to-all(f32[2,256,128]{1,0,2:T(2,128)S(1)} %pad_maximum_fusion.2), channel_id=1, replica_groups=mesh['grp'=2,'sp'=16,'sub'=8,'rep'=2] {'sub'}, dimensions={2} | all-to-all | bytes 524288 | tf_op jit(solution)/shard_map/all_to_all | solution.py:91
  149.7 0.7 slice_reduce_fusion.2
  150.4 0.5 convolution_bitcast_fusion.3
  150.9 0.5 convolution_bitcast_fusion.5
  151.4 0.5 fusion.15
  151.8 0.5 fusion.13
  152.6 0.9 pad_maximum_fusion.3
  153.5 5.8 %all-to-all-start.4 = ((f32[2,256,128]{1,0,2:T(2,128)}), f32[2,256,128]{1,0,2:T(2,128)S(1)}, u32[]{:S(2)}, u32[]{:S(2)}) async-start(f32[2,256,128]{1,0,2:T(2,128)} %pad_maximum_fusion.3), calls=%async_computation.4 | async-start | bytes 524288 | tf_op jit(solution)/shard_map/all_to_all | solution.py:97
  159.6 21.7 %all-to-all-done.4 = f32[2,256,128]{1,0,2:T(2,128)S(1)} async-done(((f32[2,256,128]{1,0,2:T(2,128)}), f32[2,256,128]{1,0,2:T(2,128)S(1)}, u32[]{:S(2)}, u32[]{:S(2)}) %all-to-all-start.4) | async-done | bytes 262176 | tf_op jit(solution)/shard_map/all_to_all | solution.py:97
  181.3 0.7 slice_reduce_fusion
  182.1 0.8 fusion.33
  182.9 0.8 fusion.238
  184.1 27.3 %all-reduce = (f32[32]{0:T(128)S(1)}, f32[32]{0:T(128)S(1)}) all-reduce(f32[32]{0:T(128)S(1)} %reduce_sum.37, f32[32]{0:T(128)S(1)} %reduce_sum.25), channel_id=1, replica_groups=mesh['grp'=2,'sp'=16,'sub'=8,'rep'=2] {'sp'}, use_global_device_ids=true, to_apply=%region_7.8 | all-reduce | flops 64 | bytes 512 | tf_op jit(solution)/shard_map/psum | solution.py:20
  211.4 14.8 %all-reduce.1 = (f32[32]{0:T(128)S(1)}, f32[32]{0:T(128)S(1)}) all-reduce(f32[32]{0:T(128)S(1)} %get-tuple-element.15, f32[32]{0:T(128)S(1)} %get-tuple-element.16), channel_id=1, replica_groups=mesh['grp'=2,'sp'=16,'sub'=8,'rep'=2] {'sub'}, use_global_device_ids=true, to_apply=%region_8.9 | all-reduce | flops 64 | bytes 512 | tf_op jit(solution)/shard_map/psum | solution.py:20
  226.1 2.5 %all-reduce.2 = (f32[32]{0:T(128)S(1)}, f32[32]{0:T(128)S(1)}) all-reduce(f32[32]{0:T(128)S(1)} %get-tuple-element.17, f32[32]{0:T(128)S(1)} %get-tuple-element.18), channel_id=1, replica_groups=mesh['grp'=2,'sp'=16,'sub'=8,'rep'=2] {'rep'}, use_global_device_ids=true, to_apply=%region_9.10 | all-reduce | flops 64 | bytes 512 | tf_op jit(solution)/shard_map/psum | solution.py:20
  229.0 0.6 copy-done.6
  229.6 0.7 copy-done.4
  230.3 0.6 copy-done.7
  230.9 0.7 fusion.22
  231.9 0.5 copy-done.5
  232.4 0.6 fusion.2
  233.0 1.0 copy.77
  (48 shorter events, 4.0 us)
Async XLA Ops:
  0.0 230.3 %copy-start = (f32[256,256]{1,0:T(8,128)S(1)}, f32[256,256]{1,0:T(8,128)}, u32[]{:S(2)}) copy-start(f32[256,256]{1,0:T(8,128)} %param.18) | copy-start | bytes 786436
  2.2 77.6 %all-to-all-start = ((f32[8,4,32,128]{3,0,1,2:T(8,128)}), f32[8,4,32,128]{3,0,1,2:T(8,128)S(1)}, u32[]{:S(2)}, u32[]{:S(2)}) async-start(f32[8,4,32,128]{3,0,1,2:T(8,128)} %copy.48), calls=%async_computation | async-start | bytes 1048576 | tf_op jit(solution)/shard_map/all_to_all | solution.py:66
  82.4 26.7 %all-to-all-start.1 = ((f32[2,256,128]{1,0,2:T(2,128)}), f32[2,256,128]{1,0,2:T(2,128)S(1)}, u32[]{:S(2)}, u32[]{:S(2)}) async-start(f32[2,256,128]{1,0,2:T(2,128)} %pad_maximum_fusion), calls=%async_computation.1 | async-start | bytes 524288 | tf_op jit(solution)/shard_map/all_to_all | solution.py:69
  112.8 8.9 %copy-start.3 = (f32[256,32]{0,1:T(8,128)S(1)}, f32[256,32]{0,1:T(8,128)}, u32[]{:S(2)}) copy-start(f32[256,32]{0,1:T(8,128)} %param.13) | copy-start | bytes 98308
  112.8 18.4 %all-to-all-start.2 = ((f32[2,256,128]{1,0,2:T(2,128)}), f32[2,256,128]{1,0,2:T(2,128)S(1)}, u32[]{:S(2)}, u32[]{:S(2)}) async-start(f32[2,256,128]{1,0,2:T(2,128)} %pad_maximum_fusion.1), calls=%async_computation.2 | async-start | bytes 524288 | tf_op jit(solution)/shard_map/all_to_all | solution.py:75
  133.4 1.0 copy-start.1
  153.5 27.8 %all-to-all-start.4 = ((f32[2,256,128]{1,0,2:T(2,128)}), f32[2,256,128]{1,0,2:T(2,128)S(1)}, u32[]{:S(2)}, u32[]{:S(2)}) async-start(f32[2,256,128]{1,0,2:T(2,128)} %pad_maximum_fusion.3), calls=%async_computation.4 | async-start | bytes 524288 | tf_op jit(solution)/shard_map/all_to_all | solution.py:97
  228.9 0.7 copy-start.6
  229.6 0.7 copy-start.4
  230.2 0.7 copy-start.7
  230.9 0.9 copy-start.2
  231.7 0.7 copy-start.5
where the time goes:
time: 236 us; the launch traced here: 234 us
  waiting for transfers between devices  86.4 us (37%)
  starting transfers between devices  62.4 us (26%)
  blocking collectives  57.5 us (24%)
  local copies, waits for them, and re-layouts  11.8 us (5%)
  matrix products  11.4 us (5%)
  other arithmetic  4.11 us (2%)
    psum x3, blocking collectives, one_axis_at_a_time(): shard = lax.psum(shard, axis)  44.5 us
    all_to_all x1, starting transfers between devices, local(): lax.all_to_all(field, ('sp', 'rep'), split_axis=2, concat_axis=0, tiled=T...  44.4 us
    all_to_all x1, waiting for transfers between devices, local(): lax.all_to_all(field, ('sp', 'rep'), split_axis=2, concat_axis=0, tiled=T...  33.1 us
    all_to_all x1, waiting for transfers between devices, local(): lax.all_to_all(planes, ('sp', 'rep'), split_axis=2, concat_axis=2, tiled=...  21.9 us
    all_to_all x1, waiting for transfers between devices, local(): lax.all_to_all(returned, ('sp', 'rep'), split_axis=2, concat_axis=2, tile...  21.7 us
    all_to_all x1, blocking collectives, local(): lax.all_to_all(returned, 'sub', split_axis=2, concat_axis=2, tiled=True)  13 us
    dot_general x21, matrix products, contract(): return jnp.einsum(formula, left, right, precision=lax.Precision.HIGHEST)  10.1 us
    all_to_all x1, waiting for transfers between devices, local(): lax.all_to_all(planes, 'sub', split_axis=2, concat_axis=2, tiled=True)  9.58 us
  transfers between devices with their start and end apart: 4, of which 4 were waited for; matrix products, arithmetic and copies ran while one was open for 1% of the time, Pallas kernels for 0%

commit v1 on v0

v1 whole, which is shorter than its diff:
```python
import math

import jax
import jax.numpy as jnp
import numpy as np
from jax import lax
from jax.experimental import pallas as pl
from jax.experimental.pallas import tpu as pltpu
from jax.sharding import PartitionSpec as P

F32 = jnp.float32
BF16 = jnp.bfloat16
GROUP_CHANNELS = 8
EPS = 1e-05


def split_np(a):
    a = np.asarray(a, np.float32)
    hi = a.astype(BF16)
    lo = (a - hi.astype(np.float32)).astype(BF16)
    return hi, lo


def build_tables(nx, ny, nz, kz, ch_local, wide):
    xl = 4
    chunks = 8
    lane = np.arange(128)
    k_of, x_of, r_of = lane // 16, (lane // 4) % 4, lane % 4
    z = np.arange(nz)
    scale = 1.0 / (nx * ny * nz)
    top = kz // 2
    fwd_z = np.zeros((xl, nz, 256))
    inv_z = np.zeros((256, xl, nz))
    for l in range(128):
        f = 2 * k_of[l] + r_of[l] // 2
        ang = 2 * np.pi * ((f * z) % nz) / nz
        fwd_z[x_of[l], :, l] = (np.cos(ang) if r_of[l] % 2 == 0 else -np.sin(ang)) * scale
        inv_z[l, x_of[l], :] = np.cos(ang) if r_of[l] % 2 == 0 else -np.sin(ang)
        if r_of[l] < 2:
            ang = 2 * np.pi * ((top * z) % nz) / nz
            col = np.cos(ang) if r_of[l] == 0 else -np.sin(ang)
            fwd_z[x_of[l], :, 128 + l] = col * scale
            inv_z[128 + l, x_of[l], :] = col
    fwd_z = fwd_z.reshape(xl * nz, 256)
    inv_z = inv_z.reshape(256, xl * nz)
    ax = np.arange(nx)
    ang = 2 * np.pi * ((ax[:, None] * ax[None, :]) % nx) / nx
    c, s = np.cos(ang), np.sin(ang)
    fwd = np.zeros((nx, 2, 2, nx, 2, 2))
    inv = np.zeros((nx, 2, 2, nx, 2, 2))
    for f in range(2):
        fwd[:, f, 0, :, f, 0] = c
        fwd[:, f, 1, :, f, 0] = s
        fwd[:, f, 0, :, f, 1] = -s
        fwd[:, f, 1, :, f, 1] = c
        inv[:, f, 0, :, f, 0] = c
        inv[:, f, 1, :, f, 0] = -s
        inv[:, f, 0, :, f, 1] = s
        inv[:, f, 1, :, f, 1] = c
    turn = np.zeros((128, 128))
    for l in range(0, 128, 2):
        turn[l + 1, l] = 1.0
        turn[l, l + 1] = -1.0
    fwd = fwd.reshape(128, 128)
    inv = inv.reshape(128, 128)
    x_fwd = np.concatenate([fwd, fwd @ turn], 1)
    x_inv = np.concatenate([inv, -(inv @ turn)], 1)
    ay = np.arange(ny)
    ang = 2 * np.pi * ((ay[:, None] * ay[None, :]) % ny) / ny
    y_tab = np.concatenate([np.cos(ang), np.sin(ang)], 1)
    hi, lo = split_np(y_tab)
    y_tab3 = np.concatenate([hi, hi, lo], 1)
    sel_x = np.zeros((nx, 256))
    for a in range(nx):
        sel_x[a, 4 * a : 4 * a + 4] = 1.0
        sel_x[a, 128 + 4 * ((nx - a) % nx) : 128 + 4 * ((nx - a) % nx) + 4] = 1.0
    sel_z = np.zeros((kz, 2, 9, nx, 4))
    for f in range(top + 1):
        k, f2 = f // 2, f % 2
        if f < top:
            sel_z[f, 0, k, :, 2 * f2 : 2 * f2 + 2] = 1.0
        if f > 0:
            sel_z[kz - f, 1, k, :, 2 * f2 : 2 * f2 + 2] = 1.0
    sel_z = sel_z.reshape(kz, 2 * 9 * 128)
    rows_in = np.arange(ch_local * ny)
    rows_out = np.arange(ch_local * 8)
    gather = (
        (rows_in[None, :] // ny == rows_out[:, None] // 8)
        & (rows_in[None, :] % 8 == rows_out[:, None] % 8)
    ).astype(np.float32)
    rows_all = np.arange(ch_local * wide)
    spread = (rows_all[:, None] // ch_local == np.arange(wide)[None, :]).astype(np.float32)
    fz = split_np(fwd_z)
    iz = split_np(inv_z)
    xf = split_np(x_fwd)
    xi = split_np(x_inv)
    return dict(
        fz_hi=fz[0], fz_lo=fz[1], iz_hi=iz[0], iz_lo=iz[1],
        xf_hi=xf[0], xf_lo=xf[1], xi_hi=xi[0], xi_lo=xi[1],
        y_tab=y_tab3,
        sel_x=sel_x.astype(np.float32), sel_z=sel_z.astype(np.float32),
        gather=gather.astype(BF16), spread=spread.astype(BF16),
    )


def split(a):
    hi = a.astype(BF16)
    return hi, (a - hi.astype(F32)).astype(BF16)


def dot1(a, b):
    return lax.dot_general(a, b, (((1,), (0,)), ((), ())), preferred_element_type=F32)


def dot3(a, b):
    return dot1(a[0], b[0]) + dot1(a[0], b[1]) + dot1(a[1], b[0])


def exact(a, b):
    return lax.dot_general(
        a, b, (((1,), (0,)), ((), ())), precision=lax.Precision.HIGHEST, preferred_element_type=F32
    )


def swap_chunks(arrays, roll):
    arrays = list(arrays)
    rows = arrays[0].shape[0]
    chunk = lax.broadcasted_iota(jnp.int32, (rows, 128), 1) // 16
    for d in (4, 2, 1):
        upper = (chunk // d) % 2 == 1
        for i in range(8):
            if (i // d) % 2 == 0:
                low, high = arrays[i], arrays[i + d]
                arrays[i] = jnp.where(upper, roll(high, 16 * d), low)
                arrays[i + d] = jnp.where(upper, high, roll(low, 128 - 16 * d))
    return arrays


def forward_z(parts, tabs):
    fz_hi, fz_lo = tabs["fz_hi"], tabs["fz_lo"]
    total = None
    for x, part in enumerate(parts):
        term = dot3(split(part), (fz_hi[128 * x : 128 * x + 128], fz_lo[128 * x : 128 * x + 128]))
        total = term if total is None else total + term
    main, extra = total[:, :128], total[:, 128:]
    rows, lanes = (lax.broadcasted_iota(jnp.int32, extra.shape, d) for d in (0, 1))
    extra = jnp.where((rows % 32) // 8 == lanes // 16, extra, 0.0)
    hi, lo = split(extra)
    packed = dot1(tabs["gather"], hi) + dot1(tabs["gather"], lo)
    return main, packed


def factor_weights(row_x, row_y, row_z, tabs):
    lanes_x = exact(row_x, tabs["sel_x"])
    lanes_z = exact(row_z, tabs["sel_z"])
    plus = lanes_z[:, :1152] * jnp.concatenate([lanes_x[:, :128]] * 9, 1)
    minus = lanes_z[:, 1152:] * jnp.concatenate([lanes_x[:, 128:]] * 9, 1)
    n = row_y.shape[1]
    r, c = (lax.broadcasted_iota(jnp.int32, (n, n), d) for d in (0, 1))
    wide = jnp.broadcast_to(row_y, (n, n))
    col_plus = jnp.sum(jnp.where(r == c, wide, 0.0), axis=1, keepdims=True)
    col_minus = jnp.sum(jnp.where((n - r) % n == c, wide, 0.0), axis=1, keepdims=True)
    return col_plus * plus + col_minus * minus


def spectral_filter(blocks, weights, tabs, roll):
    main = swap_chunks([b[:32] for b in blocks], roll)
    extra = swap_chunks([b[32:40] for b in blocks], roll)
    last = jnp.concatenate(extra[:4], 0)
    rows = jnp.concatenate(main + [last], 0)

    def along_y(pairs):
        stacked = jnp.concatenate(
            [
                jnp.concatenate(
                    [pairs[32 * k : 32 * k + 32, :128], pairs[32 * k : 32 * k + 32, 128:]], 0
                )
                for k in range(9)
            ],
            1,
        )
        hi, lo = split(stacked)
        return dot1(tabs["y_tab"], jnp.concatenate([hi, lo, hi], 0))

    pairs = dot3(split(rows), (tabs["xf_hi"], tabs["xf_lo"]))
    spec = along_y(pairs) * weights
    rows = jnp.concatenate([spec[:, 128 * k : 128 * k + 128] for k in range(9)], 0)
    pairs = dot3(split(rows), (tabs["xi_hi"], tabs["xi_lo"]))
    back = along_y(pairs)
    main = swap_chunks([back[:, 128 * k : 128 * k + 128] for k in range(8)], roll)
    last = back[:, 1024:]
    tiles = [last[8 * p : 8 * p + 8] for p in range(4)] + [jnp.zeros((8, 128), F32)] * 4
    extra = swap_chunks(tiles, roll)
    return main, extra


def leftover_rows(extras, roll):
    return jnp.concatenate(swap_chunks(extras, roll)[:4], 0)


def inverse_z(modes, left, mix, tabs):
    hi, lo = split(left)
    wide = dot1(tabs["spread"], hi) + dot1(tabs["spread"], lo)
    rows, lanes = (lax.broadcasted_iota(jnp.int32, wide.shape, d) for d in (0, 1))
    wide = jnp.where(rows % 8 == lanes // 16, wide, 0.0)
    both = jnp.concatenate([modes, wide], 1)
    mixed = dot3(mix, split(both))
    return dot3(split(mixed), (tabs["iz_hi"], tabs["iz_lo"]))


def to_column(row):
    n = row.shape[1]
    r, c = (lax.broadcasted_iota(jnp.int32, (n, n), d) for d in (0, 1))
    return jnp.sum(jnp.where(r == c, jnp.broadcast_to(row, (n, n)), 0.0), axis=1, keepdims=True)


def group_partials(total):
    folded = jnp.sum(total.reshape(total.shape[0] // 8, 8, 128), axis=1)
    return jnp.sum(folded, axis=1, keepdims=True)


def stats_row(first, second):
    n = first.shape[0]
    r, c = (lax.broadcasted_iota(jnp.int32, (n, 128), d) for d in (0, 1))
    placed = jnp.where(r == c, first, 0.0) + jnp.where(r + n == c, second, 0.0)
    return jnp.sum(placed, axis=0, keepdims=True)


def stats_columns(row, count, channels):
    groups = channels // GROUP_CHANNELS
    r, c = (lax.broadcasted_iota(jnp.int32, (channels, 128), d) for d in (0, 1))
    wide = jnp.broadcast_to(row, (channels, 128))
    first = jnp.sum(jnp.where(r // GROUP_CHANNELS == c, wide, 0.0), axis=1, keepdims=True)
    second = jnp.sum(
        jnp.where(r // GROUP_CHANNELS + groups == c, wide, 0.0), axis=1, keepdims=True
    )
    mean = first / count
    var = second / count - mean * mean
    return mean, lax.rsqrt(var + EPS)


def gelu(v):
    inner = math.sqrt(2.0 / math.pi) * (v + 0.044715 * (v * v * v))
    return 0.5 * v * (1.0 + jnp.tanh(inner))


TABLES = (
    "fz_hi", "fz_lo", "iz_hi", "iz_lo", "xf_hi", "xf_lo", "xi_hi", "xi_lo",
    "y_tab", "sel_x", "sel_z", "gather", "spread",
)
MSG = 40


class Lazy:
    def __init__(self, refs):
        self.refs = refs

    def __getitem__(self, name):
        return self.refs[name][...]


def lane_roll(a, shift):
    return pltpu.roll(a, shift, axis=1)


def fused(sizes, *refs):
    wide, narrow, channels = sizes["wide"], sizes["narrow"], sizes["channels"]
    rep = sizes["rep"]
    (field, fac_x, fac_y, fac_z, mix, gain, bias, w_in, b_in, w_out, b_out) = refs[:11]
    tabs = Lazy(dict(zip(TABLES, refs[11 : 11 + len(TABLES)])))
    out = refs[11 + len(TABLES)]
    (
        src, fld, b1, r1, b2, r2, s3, n3, s3l, n3l, st0, ar1, st1, ar2,
        wts, mix_hi, mix_lo, in_hi, in_lo, out_hi, out_lo, cols, summed, send, recv,
    ) = refs[12 + len(TABLES) :]
    me_x = lax.axis_index("sub")
    me_z = lax.axis_index(("sp", "rep"))
    channel = me_z * narrow + me_x

    def z_id(q):
        return {"sp": q // rep, "rep": q % rep}

    def x_id(s):
        return {"sub": s}

    def z_peer(j):
        step = jnp.where(j % 2 == 1, (j + 1) // 2, wide - j // 2)
        return (me_z + step) % wide

    def x_peer(j):
        return (me_x + j) % narrow

    def push(a, b, slot, where):
        pltpu.make_async_remote_copy(
            src_ref=a, dst_ref=b, send_sem=send.at[slot], recv_sem=recv.at[slot],
            device_id=where, device_id_type=pl.DeviceIdType.MESH,
        ).start()

    def drain(ref, sem):
        pltpu.make_async_copy(ref, ref, sem).wait()

    def rows(start, size):
        return pl.ds(pl.multiple_of(start, 8), size)

    barrier = pltpu.get_barrier_semaphore()

    @pl.loop(1, narrow)
    def _(j):
        pl.semaphore_signal(
            barrier, inc=1, device_id=x_id(x_peer(j)), device_id_type=pl.DeviceIdType.MESH
        )

    @pl.loop(1, wide)
    def _(j):
        pl.semaphore_signal(
            barrier, inc=1, device_id=z_id(z_peer(j)), device_id_type=pl.DeviceIdType.MESH
        )

    parts = [
        jnp.concatenate([field[128 * c + 32 * x : 128 * c + 32 * x + 32] for c in range(8)], 0)
        for x in range(4)
    ]
    main, packed = forward_z(parts, tabs)
    for c in range(8):
        b1[MSG * c : MSG * c + 32] = main[32 * c : 32 * c + 32]
        b1[MSG * c + 32 : MSG * c + 40] = packed[8 * c : 8 * c + 8]
    for y in range(32):
        src[32 * y : 32 * y + 32] = field[pl.ds(y, 32, stride=32)]

    pl.semaphore_wait(barrier, narrow - 1 + wide - 1)

    @pl.loop(1, narrow)
    def _(j):
        s = x_peer(j)
        push(b1.at[rows(s * MSG, MSG)], r1.at[rows(me_x * MSG, MSG)], 0, x_id(s))

    @pl.loop(1, wide)
    def _(j):
        q = z_peer(j)
        push(src.at[rows(q * 32, 32)], fld.at[rows(me_z * 32, 32)], 1, z_id(q))

    r1[rows(me_x * MSG, MSG)] = b1[rows(me_x * MSG, MSG)]
    fld[rows(me_z * 32, 32)] = src[rows(me_z * 32, 32)]
    one = pl.ds(channel, 1)
    wts[...] = factor_weights(fac_x[one, :], fac_y[one, :], fac_z[one, :], tabs)
    for full, hi, lo in ((mix, mix_hi, mix_lo), (w_in, in_hi, in_lo), (w_out, out_hi, out_lo)):
        hi[...], lo[...] = split(full[...])
    for n, row in enumerate((gain, bias, b_in, b_out)):
        cols[n] = jnp.broadcast_to(to_column(row[...]), (channels, 128))

    drain(r1.at[pl.ds(0, MSG * (narrow - 1))], recv.at[0])
    blocks = [r1[MSG * s : MSG * s + MSG] for s in range(8)]
    main, extra = spectral_filter(blocks, wts[...], tabs, lane_roll)
    for s in range(8):
        b2[MSG * s : MSG * s + 32] = main[s]
        b2[MSG * s + 32 : MSG * s + 40] = extra[s]

    @pl.loop(1, narrow)
    def _(j):
        s = x_peer(j)
        push(b2.at[rows(s * MSG, MSG)], r2.at[rows(me_x * MSG, MSG)], 2, x_id(s))

    r2[rows(me_x * MSG, MSG)] = b2[rows(me_x * MSG, MSG)]
    drain(r2.at[pl.ds(0, MSG * (narrow - 1))], recv.at[2])
    left = leftover_rows([r2[MSG * c + 32 : MSG * c + 40] for c in range(8)], lane_roll)
    for y in range(32):
        s3[8 * y : 8 * y + 8] = r2[pl.ds(y, 8, stride=MSG)]
        s3l[y] = left[y : y + 1]

    @pl.loop(1, wide)
    def _(j):
        q = z_peer(j)
        push(s3.at[rows(q * 8, 8)], n3.at[rows(me_z * 8, 8)], 3, z_id(q))
        push(s3l.at[q], n3l.at[me_z], 4, z_id(q))

    n3[rows(me_z * 8, 8)] = s3[rows(me_z * 8, 8)]
    n3l[me_z] = s3l[me_z]
    drain(n3.at[pl.ds(0, 8 * (wide - 1))], recv.at[3])
    drain(n3l.at[pl.ds(0, wide - 1)], recv.at[4])
    spectral = inverse_z(
        n3[...], n3l[...].reshape(wide, 128), (mix_hi[...], mix_lo[...]), tabs
    )
    drain(fld.at[pl.ds(0, 32 * (wide - 1))], recv.at[1])
    first = second = None
    for x in range(4):
        value = spectral[:, 128 * x : 128 * x + 128] + fld[pl.ds(x, channels, stride=4)]
        summed[x] = value
        first = value if x == 0 else first + value
        second = value * value if x == 0 else second + value * value
    row = stats_row(group_partials(first), group_partials(second))
    st0[0] = row
    ar1[me_z] = row

    @pl.loop(1, wide)
    def _(j):
        push(st0.at[0], ar1.at[me_z], 5, z_id(z_peer(j)))

    drain(ar1.at[pl.ds(0, wide - 1)], recv.at[5])
    row = jnp.sum(ar1[...].reshape(wide, 128), axis=0, keepdims=True)
    st1[0] = row
    ar2[me_x] = row

    @pl.loop(1, narrow)
    def _(j):
        push(st1.at[0], ar2.at[me_x], 6, x_id(x_peer(j)))

    drain(ar2.at[pl.ds(0, narrow - 1)], recv.at[6])
    row = jnp.sum(ar2[...].reshape(narrow, 128), axis=0, keepdims=True)
    mean, inv = stats_columns(row, sizes["count"], channels)
    mean = jnp.broadcast_to(mean, (channels, 128))
    scale = jnp.broadcast_to(inv, (channels, 128)) * cols[0]
    wide_in, wide_out = (in_hi[...], in_lo[...]), (out_hi[...], out_lo[...])
    for x in range(4):
        value = summed[x]
        normed = (value - mean) * scale + cols[1]
        hidden = gelu(dot3(wide_in, split(normed)) + cols[2])
        out[pl.ds(x, channels, stride=4)] = value + dot3(wide_out, split(hidden)) + cols[3]

    drain(b1.at[pl.ds(0, MSG * (narrow - 1))], send.at[0])
    drain(src.at[pl.ds(0, 32 * (wide - 1))], send.at[1])
    drain(b2.at[pl.ds(0, MSG * (narrow - 1))], send.at[2])
    drain(s3.at[pl.ds(0, 8 * (wide - 1))], send.at[3])
    drain(s3l.at[pl.ds(0, wide - 1)], send.at[4])
    drain(ar1.at[pl.ds(0, wide - 1)], send.at[5])
    drain(ar2.at[pl.ds(0, narrow - 1)], send.at[6])


def solution(mesh):
    shape = mesh.shape
    wide, narrow = shape["sp"] * shape["rep"], shape["sub"]
    replicated = P()
    placed = (P(("grp", "sp", "rep"), "sub", None, None),) + (replicated,) * 10

    def local(
        field, mix_weight, factor_x, factor_y, factor_z,
        norm_gain, norm_bias, w_in, b_in, w_out, b_out,
    ):
        held, x_local, ny, nz = field.shape
        channels = mix_weight.shape[0]
        nx = x_local * narrow
        kz = factor_z.shape[1]
        tables = build_tables(nx, ny, nz, kz, held, wide)
        sizes = dict(
            wide=wide, narrow=narrow, channels=channels, rep=shape["rep"],
            count=GROUP_CHANNELS * nx * ny * nz,
        )
        row = lambda v: v.reshape(1, -1)
        operands = [
            field.reshape(held * x_local * ny, nz), factor_x, factor_y, factor_z, mix_weight,
            row(norm_gain), row(norm_bias), w_in, row(b_in), w_out, row(b_out),
        ] + [jnp.asarray(tables[name]) for name in TABLES]
        cells = channels * x_local
        vmem = pl.BlockSpec(memory_space=pltpu.VMEM)
        f32 = lambda *dims: pltpu.VMEM(dims, F32)
        b16 = lambda *dims: pltpu.VMEM(dims, BF16)
        square = (channels, channels)
        result = pl.pallas_call(
            lambda *refs: fused(sizes, *refs),
            out_shape=jax.ShapeDtypeStruct((cells, nz), F32),
            in_specs=[vmem] * len(operands),
            out_specs=vmem,
            scratch_shapes=[
                f32(cells, nz), f32(cells, nz),
                f32(MSG * narrow, 128), f32(MSG * narrow, 128),
                f32(MSG * narrow, 128), f32(MSG * narrow, 128),
                f32(channels, 128), f32(channels, 128),
                f32(wide, 1, 128), f32(wide, 1, 128),
                f32(1, 1, 128), f32(wide, 1, 128), f32(1, 1, 128), f32(narrow, 1, 128),
                f32(ny, 9 * 128),
                b16(*square), b16(*square), b16(*square), b16(*square), b16(*square), b16(*square),
                f32(4, channels, 128), f32(x_local, channels, 128),
                pltpu.SemaphoreType.DMA((7,)), pltpu.SemaphoreType.DMA((7,)),
            ],
            compiler_params=pltpu.CompilerParams(collective_id=0, has_side_effects=True),
        )(*operands)
        return result.reshape(channels, x_local, 1, nz)

    return jax.shard_map(
        local,
        mesh=mesh,
        in_specs=placed,
        out_specs=P("grp", "sub", ("sp", "rep"), None),
        check_vma=False,
    )
```

time: 236 us -> 106 us (0.45)
  Pallas kernels: 0 us -> 100 us
  waiting for transfers between devices: 86.4 us -> 0 us
  starting transfers between devices: 62.4 us -> 0 us
  blocking collectives: 57.5 us -> 0 us
  matrix products: 11.4 us -> 0 us
  local copies, waits for them, and re-layouts: 11.8 us -> 5.22 us
  other arithmetic: 4.11 us -> 0 us
    pallas_call x0 -> x1, Pallas kernels: none -> 100 us  [local(): pl.pallas_call(lambda *refs: fused(sizes, *refs), out_shape=jax.ShapeDtyp...]
    all_to_all x4 -> x0, waiting for transfers between devices: 86.4 us -> none  [the longest x1 33.1 us: local(): lax.all_to_all(field, ('sp', 'rep'), split_axis=2, concat_axis=0, tiled=T...]
    all_to_all x4 -> x0, starting transfers between devices: 62.4 us -> none  [the longest x1 44.4 us: local(): lax.all_to_all(field, ('sp', 'rep'), split_axis=2, concat_axis=0, tiled=T...]
    psum x3 -> x0, blocking collectives: 44.5 us -> none  [one_axis_at_a_time(): shard = lax.psum(shard, axis)]
    all_to_all x1 -> x0, blocking collectives: 13 us -> none  [local(): lax.all_to_all(returned, 'sub', split_axis=2, concat_axis=2, tiled=True)]
    dot_general x23 -> x0, matrix products: 11.4 us -> none  [the longest x21 10.1 us: contract(): return jnp.einsum(formula, left, right, precision=lax.Precision.HIGHEST)]
    another operation x4 -> x0, other arithmetic: 3.07 us -> none  [the longest x3 2.12 us: transform(): return jnp.stack([real_part, imag_part])]
    slice x5 -> x0, local copies, waits for them, and re-layouts: 2.7 us -> none  [the longest x2 1.35 us: transform(): planes[1]]
  transfers between devices with their start and end apart: 4 -> 0, of which waited for: 4 -> 0; matrix products, arithmetic and copies ran while one was open for 1% -> 0% of each run, Pallas kernels for 0% -> 0%
where the time goes in v1:
time: 106 us
  Pallas kernels  100 us (94%)
  local copies, waits for them, and re-layouts  5.22 us (5%)
    pallas_call x1, Pallas kernels, local(): pl.pallas_call(lambda *refs: fused(sizes, *refs), out_shape=jax.ShapeDtyp...  100 us
    unnamed x8, local copies, waits for them, and re-layouts  5.22 us

profile of v1, /device:TPU:80, one launch (start us, length us, event | category | flops | bytes accessed | tf_op | source)
XLA Modules:
  0.0 105.7 jit_solution(1430772440150368720)
XLA Ops:
  0.0 0.0 copy-start
  0.0 1.5 %copy.25.refs_1_ = f32[256,32]{1,0:T(8,128)} copy(f32[256,32]{0,1:T(8,128)} %param.26) | data formatting | bytes 65536 | tf_op args[2]
  1.5 0.0 copy-done
  1.5 0.0 copy-start.1
  1.5 0.8 copy.26.refs_2_
  2.3 0.0 copy-done.1
  2.3 0.7 copy.27.refs_3_
  3.0 100.5 %shard_map.226 = f32[1024,128]{1,0:T(8,128)} custom-call(f32[1024,128]{1,0:T(8,128)} %bitcast.9, f32[256,32]{1,0:T(8,128)} %copy.25.refs_1_, f32[256,32]{1,0:T(8,128)} %copy.26.refs_2_, f32[256,32]{1,0:T(8,128)} %copy.27.refs_3_, f32[256,256]{1,0:T(8,128)} %refs_4_.1, f32[1,256]{1,0:T(1,128)} %bitcast.10, f32[1,256]{1,0:T(1,128)} %bitcast.11, ...), custom_call_target="tpu_custom_call" | custom-call | tf_op jit(solution)/shard_map/pallas_call | solution.py:457
  103.5 2.2 %copy.30 = f32[256,4,1,128]{3,2,1,0:T(1,128)} copy(f32[256,4,1,128]{3,2,1,0:T(1,128)} %bitcast.8) | data formatting | bytes 1048576
Async XLA Ops:
  0.0 1.5 %copy-start = (f32[256,32]{0,1:T(8,128)S(1)}, f32[256,32]{0,1:T(8,128)}, u32[]{:S(2)}) copy-start(f32[256,32]{0,1:T(8,128)} %param.27) | copy-start | bytes 98308
  1.5 0.8 copy-start.1

commit v2 on v1

--- a/solution.py
+++ b/solution.py
@@ -1,3 +1,4 @@
+import functools
 import math
 
 import jax
@@ -116,12 +117,6 @@
     return dot1(a[0], b[0]) + dot1(a[0], b[1]) + dot1(a[1], b[0])
 
 
-def exact(a, b):
-    return lax.dot_general(
-        a, b, (((1,), (0,)), ((), ())), precision=lax.Precision.HIGHEST, preferred_element_type=F32
-    )
-
-
 def swap_chunks(arrays, roll):
     arrays = list(arrays)
     rows = arrays[0].shape[0]
@@ -150,17 +145,21 @@
     return main, packed
 
 
-def factor_weights(row_x, row_y, row_z, tabs):
-    lanes_x = exact(row_x, tabs["sel_x"])
-    lanes_z = exact(row_z, tabs["sel_z"])
+def factor_weights(fac_x, fac_y, fac_z, channel, tabs):
+    n, channels = fac_y.shape
+    own = lax.broadcasted_iota(jnp.int32, (n, channels), 1) == channel
+    col_x, col_y, col_z = (
+        jnp.sum(jnp.where(own, f, 0.0), axis=1, keepdims=True) for f in (fac_x, fac_y, fac_z)
+    )
+    lanes_x = jnp.sum(col_x * tabs["sel_x"], axis=0, keepdims=True)
+    lanes_z = jnp.sum(col_z * tabs["sel_z"], axis=0, keepdims=True)
     plus = lanes_z[:, :1152] * jnp.concatenate([lanes_x[:, :128]] * 9, 1)
     minus = lanes_z[:, 1152:] * jnp.concatenate([lanes_x[:, 128:]] * 9, 1)
-    n = row_y.shape[1]
     r, c = (lax.broadcasted_iota(jnp.int32, (n, n), d) for d in (0, 1))
-    wide = jnp.broadcast_to(row_y, (n, n))
-    col_plus = jnp.sum(jnp.where(r == c, wide, 0.0), axis=1, keepdims=True)
-    col_minus = jnp.sum(jnp.where((n - r) % n == c, wide, 0.0), axis=1, keepdims=True)
-    return col_plus * plus + col_minus * minus
+    row_y = jnp.sum(jnp.where(r == c, col_y, 0.0), axis=0, keepdims=True)
+    flipped = jnp.where((n - r) % n == c, jnp.broadcast_to(row_y, (n, n)), 0.0)
+    col_minus = jnp.sum(flipped, axis=1, keepdims=True)
+    return col_y * plus + col_minus * minus
 
 
 def spectral_filter(blocks, weights, tabs, roll):
@@ -266,29 +265,38 @@
 def fused(sizes, *refs):
     wide, narrow, channels = sizes["wide"], sizes["narrow"], sizes["channels"]
     rep = sizes["rep"]
-    (field, fac_x, fac_y, fac_z, mix, gain, bias, w_in, b_in, w_out, b_out) = refs[:11]
-    tabs = Lazy(dict(zip(TABLES, refs[11 : 11 + len(TABLES)])))
-    out = refs[11 + len(TABLES)]
+    count = 5 + len(TABLES)
+    given, out = refs[:count], refs[count : count + 2]
+    scratch = refs[count + 2 :]
+    held, loaded, scratch = scratch[:count], scratch[count], scratch[count + 1 :]
+    (field, fac_x, fac_y, fac_z, mix) = held[:5]
+    tabs = Lazy(dict(zip(TABLES, held[5:])))
+    where_is = {name: 5 + n for n, name in enumerate(TABLES)}
     (
         src, fld, b1, r1, b2, r2, s3, n3, s3l, n3l, st0, ar1, st1, ar2,
-        wts, mix_hi, mix_lo, in_hi, in_lo, out_hi, out_lo, cols, summed, send, recv,
-    ) = refs[12 + len(TABLES) :]
-    me_x = lax.axis_index("sub")
-    me_z = lax.axis_index(("sp", "rep"))
+        wts, mix_hi, mix_lo, send, recv, ready,
+    ) = scratch
+    me_x, me_sp, me_rep = lax.axis_index("sub"), lax.axis_index("sp"), lax.axis_index("rep")
+    me_z = me_sp * rep + me_rep
     channel = me_z * narrow + me_x
-
-    def z_id(q):
-        return {"sp": q // rep, "rep": q % rep}
+    chips = wide // rep
+    turn = jnp.where(me_sp == 0, chips - 1, me_sp - 1)
+
+    def chip_at(position):
+        return jnp.where(position == chips - 1, 0, position + 1)
+
+    def z_id(sp, core):
+        return {"sp": sp, "rep": core}
 
     def x_id(s):
         return {"sub": s}
 
-    def z_peer(j):
-        step = jnp.where(j % 2 == 1, (j + 1) // 2, wide - j // 2)
-        return (me_z + step) % wide
-
     def x_peer(j):
-        return (me_x + j) % narrow
+        s = me_x + j
+        return jnp.where(s >= narrow, s - narrow, s)
+
+    def signal(sem, where):
+        pl.semaphore_signal(sem, inc=1, device_id=where, device_id_type=pl.DeviceIdType.MESH)
 
     def push(a, b, slot, where):
         pltpu.make_async_remote_copy(
@@ -306,16 +314,20 @@
 
     @pl.loop(1, narrow)
     def _(j):
-        pl.semaphore_signal(
-            barrier, inc=1, device_id=x_id(x_peer(j)), device_id_type=pl.DeviceIdType.MESH
-        )
-
-    @pl.loop(1, wide)
-    def _(j):
-        pl.semaphore_signal(
-            barrier, inc=1, device_id=z_id(z_peer(j)), device_id_type=pl.DeviceIdType.MESH
-        )
-
+        signal(barrier, x_id(x_peer(j)))
+
+    for core in range(1, rep):
+        signal(barrier, {"rep": (me_rep + core) % rep})
+
+    loads = [
+        pltpu.make_async_copy(a, b, loaded.at[n]) for n, (a, b) in enumerate(zip(given, held))
+    ]
+    first = [0, where_is["fz_hi"], where_is["fz_lo"], where_is["gather"]]
+    later = [n for n in range(count) if n not in first]
+    for n in first + later:
+        loads[n].start()
+    for n in first:
+        loads[n].wait()
     parts = [
         jnp.concatenate([field[128 * c + 32 * x : 128 * c + 32 * x + 32] for c in range(8)], 0)
         for x in range(4)
@@ -327,26 +339,46 @@
     for y in range(32):
         src[32 * y : 32 * y + 32] = field[pl.ds(y, 32, stride=32)]
 
-    pl.semaphore_wait(barrier, narrow - 1 + wide - 1)
+    pl.semaphore_wait(barrier, narrow - 1 + rep - 1 + rep * jnp.minimum(turn, 1))
+
+    @pl.when(turn < chips - 1)
+    def _():
+        for core in range(rep):
+            signal(barrier, z_id(chip_at(turn + 1), core))
 
     @pl.loop(1, narrow)
     def _(j):
         s = x_peer(j)
         push(b1.at[rows(s * MSG, MSG)], r1.at[rows(me_x * MSG, MSG)], 0, x_id(s))
 
-    @pl.loop(1, wide)
-    def _(j):
-        q = z_peer(j)
-        push(src.at[rows(q * 32, 32)], fld.at[rows(me_z * 32, 32)], 1, z_id(q))
+    @pl.loop(0, turn)
+    def _(position):
+        for core in range(rep):
+            signal(ready.at[me_z], z_id(chip_at(position), core))
+
+    def send_field(sp, core):
+        q = sp * rep + core
+        push(src.at[rows(q * 32, 32)], fld.at[rows(me_z * 32, 32)], 1, z_id(sp, core))
+
+    def send_modes(sp, core):
+        q = sp * rep + core
+        push(s3.at[rows(q * 8, 8)], n3.at[rows(me_z * 8, 8)], 3, z_id(sp, core))
+        push(s3l.at[q], n3l.at[me_z], 4, z_id(sp, core))
+
+    @pl.loop(0, turn)
+    def _(position):
+        for core in range(rep):
+            send_field(chip_at(position), core)
+
+    for core in range(1, rep):
+        send_field(me_sp, (me_rep + core) % rep)
 
     r1[rows(me_x * MSG, MSG)] = b1[rows(me_x * MSG, MSG)]
     fld[rows(me_z * 32, 32)] = src[rows(me_z * 32, 32)]
-    one = pl.ds(channel, 1)
-    wts[...] = factor_weights(fac_x[one, :], fac_y[one, :], fac_z[one, :], tabs)
-    for full, hi, lo in ((mix, mix_hi, mix_lo), (w_in, in_hi, in_lo), (w_out, out_hi, out_lo)):
-        hi[...], lo[...] = split(full[...])
-    for n, row in enumerate((gain, bias, b_in, b_out)):
-        cols[n] = jnp.broadcast_to(to_column(row[...]), (channels, 128))
+    for n in later:
+        loads[n].wait()
+    wts[...] = factor_weights(fac_x[...], fac_y[...], fac_z[...], channel, tabs)
+    mix_hi[...], mix_lo[...] = split(mix[...])
 
     drain(r1.at[pl.ds(0, MSG * (narrow - 1))], recv.at[0])
     blocks = [r1[MSG * s : MSG * s + MSG] for s in range(8)]
@@ -367,11 +399,21 @@
         s3[8 * y : 8 * y + 8] = r2[pl.ds(y, 8, stride=MSG)]
         s3l[y] = left[y : y + 1]
 
-    @pl.loop(1, wide)
-    def _(j):
-        q = z_peer(j)
-        push(s3.at[rows(q * 8, 8)], n3.at[rows(me_z * 8, 8)], 3, z_id(q))
-        push(s3l.at[q], n3l.at[me_z], 4, z_id(q))
+    @pl.loop(0, turn)
+    def _(position):
+        for core in range(rep):
+            send_modes(chip_at(position), core)
+
+    for core in range(1, rep):
+        send_modes(me_sp, (me_rep + core) % rep)
+
+    @pl.loop(turn + 1, chips)
+    def _(position):
+        sp = chip_at(position)
+        for core in range(rep):
+            pl.semaphore_wait(ready.at[sp * rep + core], 1)
+            send_modes(sp, core)
+            send_field(sp, core)
 
     n3[rows(me_z * 8, 8)] = s3[rows(me_z * 8, 8)]
     n3l[me_z] = s3l[me_z]
@@ -384,16 +426,20 @@
     first = second = None
     for x in range(4):
         value = spectral[:, 128 * x : 128 * x + 128] + fld[pl.ds(x, channels, stride=4)]
-        summed[x] = value
+        out[0][x] = value
         first = value if x == 0 else first + value
         second = value * value if x == 0 else second + value * value
     row = stats_row(group_partials(first), group_partials(second))
     st0[0] = row
     ar1[me_z] = row
 
-    @pl.loop(1, wide)
-    def _(j):
-        push(st0.at[0], ar1.at[me_z], 5, z_id(z_peer(j)))
+    for step in sorted(range(1, chips), key=lambda d: -min(d, chips - d)):
+        sp = me_sp + step
+        sp = jnp.where(sp >= chips, sp - chips, sp)
+        for core in range(rep):
+            push(st0.at[0], ar1.at[me_z], 5, z_id(sp, core))
+    for core in range(1, rep):
+        push(st0.at[0], ar1.at[me_z], 5, z_id(me_sp, (me_rep + core) % rep))
 
     drain(ar1.at[pl.ds(0, wide - 1)], recv.at[5])
     row = jnp.sum(ar1[...].reshape(wide, 128), axis=0, keepdims=True)
@@ -406,15 +452,7 @@
 
     drain(ar2.at[pl.ds(0, narrow - 1)], recv.at[6])
     row = jnp.sum(ar2[...].reshape(narrow, 128), axis=0, keepdims=True)
-    mean, inv = stats_columns(row, sizes["count"], channels)
-    mean = jnp.broadcast_to(mean, (channels, 128))
-    scale = jnp.broadcast_to(inv, (channels, 128)) * cols[0]
-    wide_in, wide_out = (in_hi[...], in_lo[...]), (out_hi[...], out_lo[...])
-    for x in range(4):
-        value = summed[x]
-        normed = (value - mean) * scale + cols[1]
-        hidden = gelu(dot3(wide_in, split(normed)) + cols[2])
-        out[pl.ds(x, channels, stride=4)] = value + dot3(wide_out, split(hidden)) + cols[3]
+    out[1][...] = row
 
     drain(b1.at[pl.ds(0, MSG * (narrow - 1))], send.at[0])
     drain(src.at[pl.ds(0, 32 * (wide - 1))], send.at[1])
@@ -423,6 +461,19 @@
     drain(s3l.at[pl.ds(0, wide - 1)], send.at[4])
     drain(ar1.at[pl.ds(0, wide - 1)], send.at[5])
     drain(ar2.at[pl.ds(0, narrow - 1)], send.at[6])
+
+
+def channel_mlp(count, summed, stats, gain, bias, w_in, b_in, w_out, b_out, out):
+    channels = summed.shape[1]
+    mean, inv = stats_columns(stats[...], count, channels)
+    scale = inv * to_column(gain[...])
+    shift, col_in, col_out = (to_column(v[...]) for v in (bias, b_in, b_out))
+    wide_in, wide_out = split(w_in[...]), split(w_out[...])
+    for x in range(summed.shape[0]):
+        value = summed[x]
+        normed = (value - mean) * scale + shift
+        hidden = gelu(dot3(wide_in, split(normed)) + col_in)
+        out[pl.ds(x, channels, stride=4)] = value + dot3(wide_out, split(hidden)) + col_out
 
 
 def solution(mesh):
@@ -446,20 +497,24 @@
         )
         row = lambda v: v.reshape(1, -1)
         operands = [
-            field.reshape(held * x_local * ny, nz), factor_x, factor_y, factor_z, mix_weight,
-            row(norm_gain), row(norm_bias), w_in, row(b_in), w_out, row(b_out),
+            field.reshape(held * x_local * ny, nz), factor_x.T, factor_y.T, factor_z.T, mix_weight,
         ] + [jnp.asarray(tables[name]) for name in TABLES]
         cells = channels * x_local
         vmem = pl.BlockSpec(memory_space=pltpu.VMEM)
         f32 = lambda *dims: pltpu.VMEM(dims, F32)
         b16 = lambda *dims: pltpu.VMEM(dims, BF16)
         square = (channels, channels)
-        result = pl.pallas_call(
+        summed, stats = pl.pallas_call(
             lambda *refs: fused(sizes, *refs),
-            out_shape=jax.ShapeDtypeStruct((cells, nz), F32),
-            in_specs=[vmem] * len(operands),
-            out_specs=vmem,
-            scratch_shapes=[
+            out_shape=(
+                jax.ShapeDtypeStruct((x_local, channels, nz), F32),
+                jax.ShapeDtypeStruct((1, 128), F32),
+            ),
+            in_specs=[pl.BlockSpec(memory_space=pl.ANY)] * len(operands),
+            out_specs=(vmem, vmem),
+            scratch_shapes=[pltpu.VMEM(v.shape, v.dtype) for v in operands]
+            + [pltpu.SemaphoreType.DMA((len(operands),))]
+            + [
                 f32(cells, nz), f32(cells, nz),
                 f32(MSG * narrow, 128), f32(MSG * narrow, 128),
                 f32(MSG * narrow, 128), f32(MSG * narrow, 128),
@@ -467,12 +522,18 @@
                 f32(wide, 1, 128), f32(wide, 1, 128),
                 f32(1, 1, 128), f32(wide, 1, 128), f32(1, 1, 128), f32(narrow, 1, 128),
                 f32(ny, 9 * 128),
-                b16(*square), b16(*square), b16(*square), b16(*square), b16(*square), b16(*square),
-                f32(4, channels, 128), f32(x_local, channels, 128),
+                b16(*square), b16(*square),
                 pltpu.SemaphoreType.DMA((7,)), pltpu.SemaphoreType.DMA((7,)),
+                pltpu.SemaphoreType.REGULAR((wide,)),
             ],
             compiler_params=pltpu.CompilerParams(collective_id=0, has_side_effects=True),
         )(*operands)
+        result = pl.pallas_call(
+            functools.partial(channel_mlp, sizes["count"]),
+            out_shape=jax.ShapeDtypeStruct((cells, nz), F32),
+            in_specs=[vmem] * 8,
+            out_specs=vmem,
+        )(summed, stats, row(norm_gain), row(norm_bias), w_in, row(b_in), w_out, row(b_out))
         return result.reshape(channels, x_local, 1, nz)
 
     return jax.shard_map(

time: 106 us -> 94.8 us (0.89)
  Pallas kernels: 100 us -> 94.7 us
  local copies, waits for them, and re-layouts: 5.22 us -> 0 us
    pallas_call x1 -> x2, Pallas kernels: 100 us -> 94.7 us  [the longest x1 90.8 us: local(): pl.pallas_call(lambda *refs: fused(sizes, *refs), out_shape=(jax.ShapeDty...]
    unnamed x8 -> x0, local copies, waits for them, and re-layouts: 5.22 us -> none
where the time goes in v2:
time: 94.8 us; the launch traced here: 94.7 us
  Pallas kernels  94.7 us (100%)
    pallas_call x1, Pallas kernels, local(): pl.pallas_call(lambda *refs: fused(sizes, *refs), out_shape=(jax.ShapeDty...  90.8 us
    pallas_call x1, Pallas kernels, local(): pl.pallas_call(functools.partial(channel_mlp, sizes['count']), out_shape=...  3.92 us

profile of v2, /device:TPU:80, one launch (start us, length us, event | category | flops | bytes accessed | tf_op | source)
XLA Modules:
  0.0 94.7 jit_solution(8792105743536552812)
XLA Ops:
  0.0 90.8 %shard_map.226 = (f32[4,256,128]{2,1,0:T(8,128)}, f32[1,128]{1,0:T(1,128)}) custom-call(f32[1024,128]{1,0:T(8,128)} %bitcast.11, f32[32,256]{1,0:T(8,128)} %bitcast.12, f32[32,256]{1,0:T(8,128)} %bitcast.13, f32[32,256]{1,0:T(8,128)} %bitcast.14, f32[256,256]{1,0:T(8,128)} %refs_4_.1, bf16[512,256]{1,0:T(8,128)(2,1)} %constant.26.clone.refs_5_, ...), custom_call_target="tpu_custom_call" | custom-call | tf_op jit(solution)/shard_map/pallas_call | solution.py:507
  90.8 3.9 %shard_map.227 = f32[1024,128]{1,0:T(8,128)} custom-call(f32[4,256,128]{2,1,0:T(8,128)} %get-tuple-element.7.summed, f32[1,128]{1,0:T(1,128)} %get-tuple-element.8.stats, f32[1,256]{1,0:T(1,128)} %bitcast.15, f32[1,256]{1,0:T(1,128)} %bitcast.16, f32[256,256]{1,0:T(8,128)} %w_in.1, f32[1,256]{1,0:T(1,128)} %bitcast.17, f32[256,256]{1,0:T(8,128)} %w_out.1, ...), custom_call_target="tpu_custom_call" | custom-call | tf_op jit(solution)/shard_map/pallas_call | solution.py:531

commit v3 on v2

--- a/solution.py
+++ b/solution.py
@@ -262,6 +262,13 @@
     return pltpu.roll(a, shift, axis=1)
 
 
+def far_first(n):
+    return sorted(range(1, n), key=lambda d: -min(d, n - d))
+
+
+AHEAD = 4
+
+
 def fused(sizes, *refs):
     wide, narrow, channels = sizes["wide"], sizes["narrow"], sizes["channels"]
     rep = sizes["rep"]
@@ -273,17 +280,31 @@
     tabs = Lazy(dict(zip(TABLES, held[5:])))
     where_is = {name: 5 + n for n, name in enumerate(TABLES)}
     (
-        src, fld, b1, r1, b2, r2, s3, n3, s3l, n3l, st0, ar1, st1, ar2,
+        src, fld, b1, r1, b2, r2, s3, n3, st0, ar1, st1, ar2,
         wts, mix_hi, mix_lo, send, recv, ready,
     ) = scratch
     me_x, me_sp, me_rep = lax.axis_index("sub"), lax.axis_index("sp"), lax.axis_index("rep")
     me_z = me_sp * rep + me_rep
     channel = me_z * narrow + me_x
     chips = wide // rep
-    turn = jnp.where(me_sp == 0, chips - 1, me_sp - 1)
-
-    def chip_at(position):
-        return jnp.where(position == chips - 1, 0, position + 1)
+    last = (me_sp == 0) & (me_rep == 0)
+    turn = jnp.where(last, chips, me_sp)
+
+    def each(low, high, action):
+        @pl.loop(low, high)
+        def _(position):
+            sp = jnp.where(position == chips, 0, position)
+            for core in range(rep):
+
+                @pl.when(position > 0 if core == 0 else position < chips)
+                def _():
+                    action(sp, core)
+
+    def partners(action):
+        @pl.when(me_sp > 0)
+        def _():
+            for core in range(1, rep):
+                action(me_sp, (me_rep + core) % rep)
 
     def z_id(sp, core):
         return {"sp": sp, "rep": core}
@@ -316,8 +337,7 @@
     def _(j):
         signal(barrier, x_id(x_peer(j)))
 
-    for core in range(1, rep):
-        signal(barrier, {"rep": (me_rep + core) % rep})
+    partners(lambda sp, core: signal(barrier, z_id(sp, core)))
 
     loads = [
         pltpu.make_async_copy(a, b, loaded.at[n]) for n, (a, b) in enumerate(zip(given, held))
@@ -326,6 +346,18 @@
     later = [n for n in range(count) if n not in first]
     for n in first + later:
         loads[n].start()
+    before = jnp.where(turn == 0, 0, jnp.where(turn == 1, rep - 1, rep))
+    pl.semaphore_wait(barrier, narrow - 1 + (rep - 1) * jnp.minimum(me_sp, 1) + before)
+
+    @pl.when(turn < chips - 1)
+    def _():
+        for core in range(rep):
+            signal(barrier, z_id(turn + 1, core))
+
+    @pl.when(turn == chips - 1)
+    def _():
+        signal(barrier, z_id(0, 0))
+
     for n in first:
         loads[n].wait()
     parts = [
@@ -336,25 +368,14 @@
     for c in range(8):
         b1[MSG * c : MSG * c + 32] = main[32 * c : 32 * c + 32]
         b1[MSG * c + 32 : MSG * c + 40] = packed[8 * c : 8 * c + 8]
+    for j in far_first(narrow):
+        s = x_peer(j)
+        push(b1.at[rows(s * MSG, MSG)], r1.at[rows(me_x * MSG, MSG)], 0, x_id(s))
+
     for y in range(32):
         src[32 * y : 32 * y + 32] = field[pl.ds(y, 32, stride=32)]
 
-    pl.semaphore_wait(barrier, narrow - 1 + rep - 1 + rep * jnp.minimum(turn, 1))
-
-    @pl.when(turn < chips - 1)
-    def _():
-        for core in range(rep):
-            signal(barrier, z_id(chip_at(turn + 1), core))
-
-    @pl.loop(1, narrow)
-    def _(j):
-        s = x_peer(j)
-        push(b1.at[rows(s * MSG, MSG)], r1.at[rows(me_x * MSG, MSG)], 0, x_id(s))
-
-    @pl.loop(0, turn)
-    def _(position):
-        for core in range(rep):
-            signal(ready.at[me_z], z_id(chip_at(position), core))
+    each(0, turn, lambda sp, core: signal(ready.at[me_z], z_id(sp, core)))
 
     def send_field(sp, core):
         q = sp * rep + core
@@ -362,16 +383,10 @@
 
     def send_modes(sp, core):
         q = sp * rep + core
-        push(s3.at[rows(q * 8, 8)], n3.at[rows(me_z * 8, 8)], 3, z_id(sp, core))
-        push(s3l.at[q], n3l.at[me_z], 4, z_id(sp, core))
-
-    @pl.loop(0, turn)
-    def _(position):
-        for core in range(rep):
-            send_field(chip_at(position), core)
-
-    for core in range(1, rep):
-        send_field(me_sp, (me_rep + core) % rep)
+        push(s3.at[q], n3.at[me_z], 3, z_id(sp, core))
+
+    each(0, turn, send_field)
+    partners(send_field)
 
     r1[rows(me_x * MSG, MSG)] = b1[rows(me_x * MSG, MSG)]
     fld[rows(me_z * 32, 32)] = src[rows(me_z * 32, 32)]
@@ -380,6 +395,19 @@
     wts[...] = factor_weights(fac_x[...], fac_y[...], fac_z[...], channel, tabs)
     mix_hi[...], mix_lo[...] = split(mix[...])
 
+    near = jnp.minimum(turn + 1 + AHEAD, chips + 1)
+
+    def field_when_ready(sp, core):
+        pl.semaphore_wait(ready.at[sp * rep + core], 1)
+        send_field(sp, core)
+
+    def both_when_ready(sp, core):
+        pl.semaphore_wait(ready.at[sp * rep + core], 1)
+        send_modes(sp, core)
+        send_field(sp, core)
+
+    each(turn + 1, near, field_when_ready)
+
     drain(r1.at[pl.ds(0, MSG * (narrow - 1))], recv.at[0])
     blocks = [r1[MSG * s : MSG * s + MSG] for s in range(8)]
     main, extra = spectral_filter(blocks, wts[...], tabs, lane_roll)
@@ -387,8 +415,7 @@
         b2[MSG * s : MSG * s + 32] = main[s]
         b2[MSG * s + 32 : MSG * s + 40] = extra[s]
 
-    @pl.loop(1, narrow)
-    def _(j):
+    for j in far_first(narrow):
         s = x_peer(j)
         push(b2.at[rows(s * MSG, MSG)], r2.at[rows(me_x * MSG, MSG)], 2, x_id(s))
 
@@ -396,31 +423,18 @@
     drain(r2.at[pl.ds(0, MSG * (narrow - 1))], recv.at[2])
     left = leftover_rows([r2[MSG * c + 32 : MSG * c + 40] for c in range(8)], lane_roll)
     for y in range(32):
-        s3[8 * y : 8 * y + 8] = r2[pl.ds(y, 8, stride=MSG)]
-        s3l[y] = left[y : y + 1]
-
-    @pl.loop(0, turn)
-    def _(position):
-        for core in range(rep):
-            send_modes(chip_at(position), core)
-
-    for core in range(1, rep):
-        send_modes(me_sp, (me_rep + core) % rep)
-
-    @pl.loop(turn + 1, chips)
-    def _(position):
-        sp = chip_at(position)
-        for core in range(rep):
-            pl.semaphore_wait(ready.at[sp * rep + core], 1)
-            send_modes(sp, core)
-            send_field(sp, core)
-
-    n3[rows(me_z * 8, 8)] = s3[rows(me_z * 8, 8)]
-    n3l[me_z] = s3l[me_z]
-    drain(n3.at[pl.ds(0, 8 * (wide - 1))], recv.at[3])
-    drain(n3l.at[pl.ds(0, wide - 1)], recv.at[4])
+        s3[y, :8] = r2[pl.ds(y, 8, stride=MSG)]
+        s3[y, 8:] = left[y : y + 1]
+
+    each(0, turn, send_modes)
+    partners(send_modes)
+    each(turn + 1, near, send_modes)
+    each(near, chips + 1, both_when_ready)
+
+    n3[me_z] = s3[me_z]
+    drain(n3.at[pl.ds(0, wide - 1)], recv.at[3])
     spectral = inverse_z(
-        n3[...], n3l[...].reshape(wide, 128), (mix_hi[...], mix_lo[...]), tabs
+        n3[:, :8].reshape(channels, 128), n3[:, 8:].reshape(wide, 128), (mix_hi[...], mix_lo[...]), tabs
     )
     drain(fld.at[pl.ds(0, 32 * (wide - 1))], recv.at[1])
     first = second = None
@@ -433,7 +447,7 @@
     st0[0] = row
     ar1[me_z] = row
 
-    for step in sorted(range(1, chips), key=lambda d: -min(d, chips - d)):
+    for step in far_first(chips):
         sp = me_sp + step
         sp = jnp.where(sp >= chips, sp - chips, sp)
         for core in range(rep):
@@ -446,8 +460,7 @@
     st1[0] = row
     ar2[me_x] = row
 
-    @pl.loop(1, narrow)
-    def _(j):
+    for j in far_first(narrow):
         push(st1.at[0], ar2.at[me_x], 6, x_id(x_peer(j)))
 
     drain(ar2.at[pl.ds(0, narrow - 1)], recv.at[6])
@@ -457,8 +470,7 @@
     drain(b1.at[pl.ds(0, MSG * (narrow - 1))], send.at[0])
     drain(src.at[pl.ds(0, 32 * (wide - 1))], send.at[1])
     drain(b2.at[pl.ds(0, MSG * (narrow - 1))], send.at[2])
-    drain(s3.at[pl.ds(0, 8 * (wide - 1))], send.at[3])
-    drain(s3l.at[pl.ds(0, wide - 1)], send.at[4])
+    drain(s3.at[pl.ds(0, wide - 1)], send.at[3])
     drain(ar1.at[pl.ds(0, wide - 1)], send.at[5])
     drain(ar2.at[pl.ds(0, narrow - 1)], send.at[6])
 
@@ -510,7 +522,7 @@
                 jax.ShapeDtypeStruct((x_local, channels, nz), F32),
                 jax.ShapeDtypeStruct((1, 128), F32),
             ),
-            in_specs=[pl.BlockSpec(memory_space=pl.ANY)] * len(operands),
+            in_specs=[pl.BlockSpec(memory_space=pltpu.HBM)] * len(operands),
             out_specs=(vmem, vmem),
             scratch_shapes=[pltpu.VMEM(v.shape, v.dtype) for v in operands]
             + [pltpu.SemaphoreType.DMA((len(operands),))]
@@ -518,21 +530,23 @@
                 f32(cells, nz), f32(cells, nz),
                 f32(MSG * narrow, 128), f32(MSG * narrow, 128),
                 f32(MSG * narrow, 128), f32(MSG * narrow, 128),
-                f32(channels, 128), f32(channels, 128),
-                f32(wide, 1, 128), f32(wide, 1, 128),
+                f32(wide, 9, 128), f32(wide, 9, 128),
                 f32(1, 1, 128), f32(wide, 1, 128), f32(1, 1, 128), f32(narrow, 1, 128),
                 f32(ny, 9 * 128),
                 b16(*square), b16(*square),
                 pltpu.SemaphoreType.DMA((7,)), pltpu.SemaphoreType.DMA((7,)),
                 pltpu.SemaphoreType.REGULAR((wide,)),
             ],
-            compiler_params=pltpu.CompilerParams(collective_id=0, has_side_effects=True),
-        )(*operands)
+            compiler_params=pltpu.CompilerParams(
+                collective_id=0, has_side_effects=True, vmem_limit_bytes=24 * 2**20
+            ),
+        )(*[pltpu.with_memory_space_constraint(v, pltpu.HBM) for v in operands])
         result = pl.pallas_call(
             functools.partial(channel_mlp, sizes["count"]),
             out_shape=jax.ShapeDtypeStruct((cells, nz), F32),
             in_specs=[vmem] * 8,
             out_specs=vmem,
+            compiler_params=pltpu.CompilerParams(vmem_limit_bytes=24 * 2**20),
         )(summed, stats, row(norm_gain), row(norm_bias), w_in, row(b_in), w_out, row(b_out))
         return result.reshape(channels, x_local, 1, nz)
 

time: 94.8 us -> 91.3 us (0.963)
  Pallas kernels: 94.7 us -> 90.5 us
    pallas_call x1, Pallas kernels: 90.8 us -> 87.8 us  [local(): pl.pallas_call(lambda *refs: fused(sizes, *refs), out_shape=(jax.ShapeDty...]
    pallas_call x1, Pallas kernels: 3.92 us -> 2.67 us  [local(): pl.pallas_call(functools.partial(channel_mlp, sizes['count']), out_shape=...]
where the time goes in v3:
time: 91.3 us; the launch traced here: 91.2 us
  Pallas kernels  90.5 us (99%)
    pallas_call x1, Pallas kernels, local(): pl.pallas_call(lambda *refs: fused(sizes, *refs), out_shape=(jax.ShapeDty...  87.8 us
    pallas_call x1, Pallas kernels, local(): pl.pallas_call(functools.partial(channel_mlp, sizes['count']), out_shape=...  2.67 us

profile of v3, /device:TPU:80, one launch (start us, length us, event | category | flops | bytes accessed | tf_op | source)
XLA Modules:
  0.0 91.2 jit_solution(9670893839187470204)
XLA Ops:
  0.0 0.0 copy-start
  0.0 0.0 copy-start.1
  0.0 0.0 copy-start.3
  0.0 0.0 copy-start.4
  0.0 0.0 copy-start.5
  0.0 87.8 %shard_map.226 = (f32[4,256,128]{2,1,0:T(8,128)S(1)}, f32[1,128]{1,0:T(1,128)S(1)}) custom-call(f32[1024,128]{1,0:T(8,128)} %bitcast.15, f32[32,256]{1,0:T(8,128)} %bitcast.16, f32[32,256]{1,0:T(8,128)} %bitcast.17, f32[32,256]{1,0:T(8,128)} %bitcast.18, f32[256,256]{1,0:T(8,128)} %refs_4_.1, bf16[512,256]{1,0:T(8,128)(2,1)} %constant.26.clone.refs_5_, ...), custom_call_target="tpu_custom_call" | custom-call | tf_op jit(solution)/shard_map/pallas_call | solution.py:519
  87.8 0.0 copy-start.2
  87.8 0.0 copy-done
  87.8 0.0 copy-done.1
  87.9 0.0 copy-done.3
  87.9 0.0 copy-done.4
  87.9 0.0 copy-done.5
  87.9 0.6 copy-done.2
  88.5 2.7 %shard_map.227 = f32[1024,128]{1,0:T(8,128)} custom-call(f32[4,256,128]{2,1,0:T(8,128)S(1)} %get-tuple-element.7.summed, f32[1,128]{1,0:T(1,128)S(1)} %get-tuple-element.8.stats, f32[1,256]{1,0:T(1,128)S(1)} %bitcast.11, f32[1,256]{1,0:T(1,128)S(1)} %bitcast.12, f32[256,256]{1,0:T(8,128)S(1)} %copy-done, f32[1,256]{1,0:T(1,128)S(1)} %bitcast.13, ...), custom_call_target="tpu_custom_call" | custom-call | tf_op jit(solution)/shard_map/pallas_call | solution.py:544
Async XLA Ops:
  0.0 87.8 %copy-start = (f32[256,256]{1,0:T(8,128)S(1)}, f32[256,256]{1,0:T(8,128)}, u32[]{:S(2)}) copy-start(f32[256,256]{1,0:T(8,128)} %w_in.1) | copy-start | bytes 786436
  0.0 87.8 %copy-start.1 = (f32[256,256]{1,0:T(8,128)S(1)}, f32[256,256]{1,0:T(8,128)}, u32[]{:S(2)}) copy-start(f32[256,256]{1,0:T(8,128)} %w_out.1) | copy-start | bytes 786436
  0.0 87.8 %copy-start.3 = (f32[256]{0:T(256)S(1)}, f32[256]{0:T(256)}, u32[]{:S(2)}) copy-start(f32[256]{0:T(256)} %param.30) | copy-start | bytes 3076
  0.0 87.9 %copy-start.4 = (f32[256]{0:T(256)S(1)}, f32[256]{0:T(256)}, u32[]{:S(2)}) copy-start(f32[256]{0:T(256)} %param.32) | copy-start | bytes 3076
  0.0 87.9 %copy-start.5 = (f32[256]{0:T(256)S(1)}, f32[256]{0:T(256)}, u32[]{:S(2)}) copy-start(f32[256]{0:T(256)} %param.34) | copy-start | bytes 3076
  87.8 0.7 copy-start.2

commit v4 on v3

--- a/solution.py
+++ b/solution.py
@@ -346,6 +346,20 @@
     later = [n for n in range(count) if n not in first]
     for n in first + later:
         loads[n].start()
+    def own_modes(waits):
+        for n in waits:
+            loads[n].wait()
+        parts = [
+            jnp.concatenate([field[128 * c + 32 * x : 128 * c + 32 * x + 32] for c in range(8)], 0)
+            for x in range(4)
+        ]
+        main, packed = forward_z(parts, tabs)
+        for c in range(8):
+            b1[MSG * c : MSG * c + 32] = main[32 * c : 32 * c + 32]
+            b1[MSG * c + 32 : MSG * c + 40] = packed[8 * c : 8 * c + 8]
+
+    pl.when(turn == chips)(lambda: own_modes(first))
+
     before = jnp.where(turn == 0, 0, jnp.where(turn == 1, rep - 1, rep))
     pl.semaphore_wait(barrier, narrow - 1 + (rep - 1) * jnp.minimum(me_sp, 1) + before)
 
@@ -358,35 +372,37 @@
     def _():
         signal(barrier, z_id(0, 0))
 
-    for n in first:
-        loads[n].wait()
-    parts = [
-        jnp.concatenate([field[128 * c + 32 * x : 128 * c + 32 * x + 32] for c in range(8)], 0)
-        for x in range(4)
-    ]
-    main, packed = forward_z(parts, tabs)
-    for c in range(8):
-        b1[MSG * c : MSG * c + 32] = main[32 * c : 32 * c + 32]
-        b1[MSG * c + 32 : MSG * c + 40] = packed[8 * c : 8 * c + 8]
+    def send_field(sp, core):
+        q = sp * rep + core
+        push(src.at[rows(q * 32, 32)], fld.at[rows(me_z * 32, 32)], 1, z_id(sp, core))
+
+    def spread_field():
+        for y in range(32):
+            src[32 * y : 32 * y + 32] = field[pl.ds(y, 32, stride=32)]
+        each(0, turn, send_field)
+        partners(send_field)
+
+    def tell_before():
+        each(0, turn, lambda sp, core: signal(ready.at[me_z], z_id(sp, core)))
+
+    @pl.when(turn < chips)
+    def _():
+        tell_before()
+        for n in first[:1]:
+            loads[n].wait()
+        pl.when(turn < chips - 1)(spread_field)
+        own_modes(first[1:])
+
     for j in far_first(narrow):
         s = x_peer(j)
         push(b1.at[rows(s * MSG, MSG)], r1.at[rows(me_x * MSG, MSG)], 0, x_id(s))
 
-    for y in range(32):
-        src[32 * y : 32 * y + 32] = field[pl.ds(y, 32, stride=32)]
-
-    each(0, turn, lambda sp, core: signal(ready.at[me_z], z_id(sp, core)))
-
-    def send_field(sp, core):
-        q = sp * rep + core
-        push(src.at[rows(q * 32, 32)], fld.at[rows(me_z * 32, 32)], 1, z_id(sp, core))
-
     def send_modes(sp, core):
         q = sp * rep + core
         push(s3.at[q], n3.at[me_z], 3, z_id(sp, core))
 
-    each(0, turn, send_field)
-    partners(send_field)
+    pl.when(turn == chips)(tell_before)
+    pl.when(turn >= chips - 1)(spread_field)
 
     r1[rows(me_x * MSG, MSG)] = b1[rows(me_x * MSG, MSG)]
     fld[rows(me_z * 32, 32)] = src[rows(me_z * 32, 32)]
@@ -426,10 +442,21 @@
         s3[y, :8] = r2[pl.ds(y, 8, stride=MSG)]
         s3[y, 8:] = left[y : y + 1]
 
-    each(0, turn, send_modes)
-    partners(send_modes)
-    each(turn + 1, near, send_modes)
-    each(near, chips + 1, both_when_ready)
+    @pl.when(near == chips + 1)
+    def _():
+        for step in far_first(chips):
+            sp = me_sp + step
+            for core in range(rep):
+                send_modes(jnp.where(sp >= chips, sp - chips, sp), core)
+        for core in range(1, rep):
+            send_modes(me_sp, (me_rep + core) % rep)
+
+    @pl.when(near < chips + 1)
+    def _():
+        each(0, turn, send_modes)
+        partners(send_modes)
+        each(turn + 1, near, send_modes)
+        each(near, chips + 1, both_when_ready)
 
     n3[me_z] = s3[me_z]
     drain(n3.at[pl.ds(0, wide - 1)], recv.at[3])

time: 91.3 us -> 89.9 us (0.985)
  Pallas kernels: 90.5 us -> 89 us
    pallas_call x1, Pallas kernels: 87.8 us -> 86.3 us  [local(): pl.pallas_call(lambda *refs: fused(sizes, *refs), out_shape=(jax.ShapeDty...]
where the time goes in v4:
time: 89.9 us; the launch traced here: 89.7 us
  Pallas kernels  89 us (99%)
    pallas_call x1, Pallas kernels, local(): pl.pallas_call(lambda *refs: fused(sizes, *refs), out_shape=(jax.ShapeDty...  86.3 us
    pallas_call x1, Pallas kernels, local(): pl.pallas_call(functools.partial(channel_mlp, sizes['count']), out_shape=...  2.68 us

profile of v4, /device:TPU:80, one launch (start us, length us, event | category | flops | bytes accessed | tf_op | source)
XLA Modules:
  0.0 89.7 jit_solution(3471618863875413306)
XLA Ops:
  0.0 0.0 copy-start
  0.0 0.0 copy-start.1
  0.0 0.0 copy-start.3
  0.0 0.0 copy-start.4
  0.0 0.0 copy-start.5
  0.0 86.3 %shard_map.226 = (f32[4,256,128]{2,1,0:T(8,128)S(1)}, f32[1,128]{1,0:T(1,128)S(1)}) custom-call(f32[1024,128]{1,0:T(8,128)} %bitcast.15, f32[32,256]{1,0:T(8,128)} %bitcast.16, f32[32,256]{1,0:T(8,128)} %bitcast.17, f32[32,256]{1,0:T(8,128)} %bitcast.18, f32[256,256]{1,0:T(8,128)} %refs_4_.1, bf16[512,256]{1,0:T(8,128)(2,1)} %constant.26.clone.refs_5_, ...), custom_call_target="tpu_custom_call" | custom-call | tf_op jit(solution)/shard_map/pallas_call | solution.py:546
  86.4 0.0 copy-start.2
  86.4 0.0 copy-done
  86.4 0.0 copy-done.1
  86.4 0.0 copy-done.3
  86.4 0.0 copy-done.4
  86.4 0.0 copy-done.5
  86.4 0.6 copy-done.2
  87.0 2.7 %shard_map.227 = f32[1024,128]{1,0:T(8,128)} custom-call(f32[4,256,128]{2,1,0:T(8,128)S(1)} %get-tuple-element.7.summed, f32[1,128]{1,0:T(1,128)S(1)} %get-tuple-element.8.stats, f32[1,256]{1,0:T(1,128)S(1)} %bitcast.11, f32[1,256]{1,0:T(1,128)S(1)} %bitcast.12, f32[256,256]{1,0:T(8,128)S(1)} %copy-done, f32[1,256]{1,0:T(1,128)S(1)} %bitcast.13, ...), custom_call_target="tpu_custom_call" | custom-call | tf_op jit(solution)/shard_map/pallas_call | solution.py:571
Async XLA Ops:
  0.0 86.4 %copy-start = (f32[256,256]{1,0:T(8,128)S(1)}, f32[256,256]{1,0:T(8,128)}, u32[]{:S(2)}) copy-start(f32[256,256]{1,0:T(8,128)} %w_in.1) | copy-start | bytes 786436
  0.0 86.4 %copy-start.1 = (f32[256,256]{1,0:T(8,128)S(1)}, f32[256,256]{1,0:T(8,128)}, u32[]{:S(2)}) copy-start(f32[256,256]{1,0:T(8,128)} %w_out.1) | copy-start | bytes 786436
  0.0 86.4 %copy-start.3 = (f32[256]{0:T(256)S(1)}, f32[256]{0:T(256)}, u32[]{:S(2)}) copy-start(f32[256]{0:T(256)} %param.30) | copy-start | bytes 3076
  0.0 86.4 %copy-start.4 = (f32[256]{0:T(256)S(1)}, f32[256]{0:T(256)}, u32[]{:S(2)}) copy-start(f32[256]{0:T(256)} %param.32) | copy-start | bytes 3076
  0.0 86.4 %copy-start.5 = (f32[256]{0:T(256)S(1)}, f32[256]{0:T(256)}, u32[]{:S(2)}) copy-start(f32[256]{0:T(256)} %param.34) | copy-start | bytes 3076
  86.4 0.7 copy-start.2

commit v5 on v4

--- a/solution.py
+++ b/solution.py
@@ -272,13 +272,13 @@
 def fused(sizes, *refs):
     wide, narrow, channels = sizes["wide"], sizes["narrow"], sizes["channels"]
     rep = sizes["rep"]
-    count = 5 + len(TABLES)
-    given, out = refs[:count], refs[count : count + 2]
-    scratch = refs[count + 2 :]
+    count = 11 + len(TABLES)
+    given, out = refs[:count], refs[count : count + 7]
+    scratch = refs[count + 7 :]
     held, loaded, scratch = scratch[:count], scratch[count], scratch[count + 1 :]
-    (field, fac_x, fac_y, fac_z, mix) = held[:5]
-    tabs = Lazy(dict(zip(TABLES, held[5:])))
-    where_is = {name: 5 + n for n, name in enumerate(TABLES)}
+    (field, fac_x, fac_y, fac_z, mix, gain, bias, w_in, b_in, w_out, b_out) = held[:11]
+    tabs = Lazy(dict(zip(TABLES, held[11:])))
+    where_is = {name: 11 + n for n, name in enumerate(TABLES)}
     (
         src, fld, b1, r1, b2, r2, s3, n3, st0, ar1, st1, ar2,
         wts, mix_hi, mix_lo, send, recv, ready,
@@ -409,7 +409,10 @@
     for n in later:
         loads[n].wait()
     wts[...] = factor_weights(fac_x[...], fac_y[...], fac_z[...], channel, tabs)
-    mix_hi[...], mix_lo[...] = split(mix[...])
+    for full, hi, lo in ((mix, mix_hi, mix_lo), (w_in, *out[3:5]), (w_out, *out[5:7])):
+        hi[...], lo[...] = split(full[...])
+    for n, row in enumerate((gain, bias, b_in, b_out)):
+        out[2][n] = jnp.broadcast_to(to_column(row[...]), (channels, 128))
 
     near = jnp.minimum(turn + 1 + AHEAD, chips + 1)
 
@@ -502,17 +505,17 @@
     drain(ar2.at[pl.ds(0, narrow - 1)], send.at[6])
 
 
-def channel_mlp(count, summed, stats, gain, bias, w_in, b_in, w_out, b_out, out):
+def channel_mlp(count, summed, stats, cols, in_hi, in_lo, out_hi, out_lo, out):
     channels = summed.shape[1]
     mean, inv = stats_columns(stats[...], count, channels)
-    scale = inv * to_column(gain[...])
-    shift, col_in, col_out = (to_column(v[...]) for v in (bias, b_in, b_out))
-    wide_in, wide_out = split(w_in[...]), split(w_out[...])
+    mean = jnp.broadcast_to(mean, (channels, 128))
+    scale = jnp.broadcast_to(inv, (channels, 128)) * cols[0]
+    wide_in, wide_out = (in_hi[...], in_lo[...]), (out_hi[...], out_lo[...])
     for x in range(summed.shape[0]):
         value = summed[x]
-        normed = (value - mean) * scale + shift
-        hidden = gelu(dot3(wide_in, split(normed)) + col_in)
-        out[pl.ds(x, channels, stride=4)] = value + dot3(wide_out, split(hidden)) + col_out
+        normed = (value - mean) * scale + cols[1]
+        hidden = gelu(dot3(wide_in, split(normed)) + cols[2])
+        out[pl.ds(x, channels, stride=4)] = value + dot3(wide_out, split(hidden)) + cols[3]
 
 
 def solution(mesh):
@@ -537,20 +540,23 @@
         row = lambda v: v.reshape(1, -1)
         operands = [
             field.reshape(held * x_local * ny, nz), factor_x.T, factor_y.T, factor_z.T, mix_weight,
+            row(norm_gain), row(norm_bias), w_in, row(b_in), w_out, row(b_out),
         ] + [jnp.asarray(tables[name]) for name in TABLES]
         cells = channels * x_local
         vmem = pl.BlockSpec(memory_space=pltpu.VMEM)
         f32 = lambda *dims: pltpu.VMEM(dims, F32)
         b16 = lambda *dims: pltpu.VMEM(dims, BF16)
         square = (channels, channels)
-        summed, stats = pl.pallas_call(
+        handed = pl.pallas_call(
             lambda *refs: fused(sizes, *refs),
             out_shape=(
                 jax.ShapeDtypeStruct((x_local, channels, nz), F32),
                 jax.ShapeDtypeStruct((1, 128), F32),
-            ),
+                jax.ShapeDtypeStruct((4, channels, 128), F32),
+            )
+            + (jax.ShapeDtypeStruct(square, BF16),) * 4,
             in_specs=[pl.BlockSpec(memory_space=pltpu.HBM)] * len(operands),
-            out_specs=(vmem, vmem),
+            out_specs=(vmem,) * 7,
             scratch_shapes=[pltpu.VMEM(v.shape, v.dtype) for v in operands]
             + [pltpu.SemaphoreType.DMA((len(operands),))]
             + [
@@ -571,10 +577,10 @@
         result = pl.pallas_call(
             functools.partial(channel_mlp, sizes["count"]),
             out_shape=jax.ShapeDtypeStruct((cells, nz), F32),
-            in_specs=[vmem] * 8,
+            in_specs=[vmem] * 7,
             out_specs=vmem,
             compiler_params=pltpu.CompilerParams(vmem_limit_bytes=24 * 2**20),
-        )(summed, stats, row(norm_gain), row(norm_bias), w_in, row(b_in), w_out, row(b_out))
+        )(*handed)
         return result.reshape(channels, x_local, 1, nz)
 
     return jax.shard_map(

time: 89.9 us -> 89 us (0.990)
  no operation moved by 1% of the time
where the time goes in v5:
time: 89 us; the launch traced here: 88.8 us
  Pallas kernels  88.8 us (100%)
    pallas_call x1, Pallas kernels, local(): pl.pallas_call(lambda *refs: fused(sizes, *refs), out_shape=(jax.ShapeDty...  86.2 us
    pallas_call x1, Pallas kernels, local(): pl.pallas_call(functools.partial(channel_mlp, sizes['count']), out_shape=...  2.63 us

profile of v5, /device:TPU:80, one launch (start us, length us, event | category | flops | bytes accessed | tf_op | source)
XLA Modules:
  0.0 88.8 jit_solution(17827757088226048158)
XLA Ops:
  0.0 86.2 %shard_map.226 = (f32[4,256,128]{2,1,0:T(8,128)S(1)}, f32[1,128]{1,0:T(1,128)S(1)}, f32[4,256,128]{2,1,0:T(8,128)S(1)}, bf16[256,256]{1,0:T(8,128)(2,1)S(1)}, bf...) custom-call(f32[1024,128]{1,0:T(8,128)} %bitcast.11, f32[32,256]{1,0:T(8,128)} %bitcast.12, ...), custom_call_target="tpu_custom_call" | custom-call | tf_op jit(solution)/shard_map/pallas_call | solution.py:550
  86.2 2.6 %shard_map.227 = f32[1024,128]{1,0:T(8,128)} custom-call(f32[4,256,128]{2,1,0:T(8,128)S(1)} %get-tuple-element.12.summed, f32[1,128]{1,0:T(1,128)S(1)} %get-tuple-element.13.stats, f32[4,256,128]{2,1,0:T(8,128)S(1)} %get-tuple-element.14.cols, bf16[256,256]{1,0:T(8,128)(2,1)S(1)} %get-tuple-element.15.in_hi, bf16[256,256]{1,0:T(8,128)(2,1)S(1)} %get-tuple-element.16.in_lo, ...), custom_call_target="tpu_custom_call" | custom-call | tf_op jit(solution)/shard_map/pallas_call | solution.py:577

commit v6 on v5

--- a/solution.py
+++ b/solution.py
@@ -247,7 +247,7 @@
     "fz_hi", "fz_lo", "iz_hi", "iz_lo", "xf_hi", "xf_lo", "xi_hi", "xi_lo",
     "y_tab", "sel_x", "sel_z", "gather", "spread",
 )
-MSG = 40
+MSG = 36
 
 
 class Lazy:
@@ -260,6 +260,14 @@
 
 def lane_roll(a, shift):
     return pltpu.roll(a, shift, axis=1)
+
+
+def fold(tile):
+    return tile[:4] + lane_roll(tile[4:], 64)
+
+
+def unfold(tile):
+    return jnp.concatenate([tile, lane_roll(tile, 64)], 0)
 
 
 def far_first(n):
@@ -355,8 +363,8 @@
         ]
         main, packed = forward_z(parts, tabs)
         for c in range(8):
-            b1[MSG * c : MSG * c + 32] = main[32 * c : 32 * c + 32]
-            b1[MSG * c + 32 : MSG * c + 40] = packed[8 * c : 8 * c + 8]
+            b1[c, :32] = main[32 * c : 32 * c + 32]
+            b1[c, 32:] = fold(packed[8 * c : 8 * c + 8])
 
     pl.when(turn == chips)(lambda: own_modes(first))
 
@@ -395,7 +403,7 @@
 
     for j in far_first(narrow):
         s = x_peer(j)
-        push(b1.at[rows(s * MSG, MSG)], r1.at[rows(me_x * MSG, MSG)], 0, x_id(s))
+        push(b1.at[s], r1.at[me_x], 0, x_id(s))
 
     def send_modes(sp, core):
         q = sp * rep + core
@@ -404,7 +412,7 @@
     pl.when(turn == chips)(tell_before)
     pl.when(turn >= chips - 1)(spread_field)
 
-    r1[rows(me_x * MSG, MSG)] = b1[rows(me_x * MSG, MSG)]
+    r1[me_x] = b1[me_x]
     fld[rows(me_z * 32, 32)] = src[rows(me_z * 32, 32)]
     for n in later:
         loads[n].wait()
@@ -427,22 +435,22 @@
 
     each(turn + 1, near, field_when_ready)
 
-    drain(r1.at[pl.ds(0, MSG * (narrow - 1))], recv.at[0])
-    blocks = [r1[MSG * s : MSG * s + MSG] for s in range(8)]
+    drain(r1.at[pl.ds(0, narrow - 1)], recv.at[0])
+    blocks = [jnp.concatenate([r1[s, :32], unfold(r1[s, 32:])], 0) for s in range(8)]
     main, extra = spectral_filter(blocks, wts[...], tabs, lane_roll)
     for s in range(8):
-        b2[MSG * s : MSG * s + 32] = main[s]
-        b2[MSG * s + 32 : MSG * s + 40] = extra[s]
+        b2[s, :32] = main[s]
+        b2[s, 32:] = fold(extra[s])
 
     for j in far_first(narrow):
         s = x_peer(j)
-        push(b2.at[rows(s * MSG, MSG)], r2.at[rows(me_x * MSG, MSG)], 2, x_id(s))
-
-    r2[rows(me_x * MSG, MSG)] = b2[rows(me_x * MSG, MSG)]
-    drain(r2.at[pl.ds(0, MSG * (narrow - 1))], recv.at[2])
-    left = leftover_rows([r2[MSG * c + 32 : MSG * c + 40] for c in range(8)], lane_roll)
+        push(b2.at[s], r2.at[me_x], 2, x_id(s))
+
+    r2[me_x] = b2[me_x]
+    drain(r2.at[pl.ds(0, narrow - 1)], recv.at[2])
+    left = leftover_rows([unfold(r2[c, 32:]) for c in range(8)], lane_roll)
     for y in range(32):
-        s3[y, :8] = r2[pl.ds(y, 8, stride=MSG)]
+        s3[y, :8] = r2[:, y]
         s3[y, 8:] = left[y : y + 1]
 
     @pl.when(near == chips + 1)
@@ -497,9 +505,9 @@
     row = jnp.sum(ar2[...].reshape(narrow, 128), axis=0, keepdims=True)
     out[1][...] = row
 
-    drain(b1.at[pl.ds(0, MSG * (narrow - 1))], send.at[0])
+    drain(b1.at[pl.ds(0, narrow - 1)], send.at[0])
     drain(src.at[pl.ds(0, 32 * (wide - 1))], send.at[1])
-    drain(b2.at[pl.ds(0, MSG * (narrow - 1))], send.at[2])
+    drain(b2.at[pl.ds(0, narrow - 1)], send.at[2])
     drain(s3.at[pl.ds(0, wide - 1)], send.at[3])
     drain(ar1.at[pl.ds(0, wide - 1)], send.at[5])
     drain(ar2.at[pl.ds(0, narrow - 1)], send.at[6])
@@ -561,8 +569,8 @@
             + [pltpu.SemaphoreType.DMA((len(operands),))]
             + [
                 f32(cells, nz), f32(cells, nz),
-                f32(MSG * narrow, 128), f32(MSG * narrow, 128),
-                f32(MSG * narrow, 128), f32(MSG * narrow, 128),
+                f32(narrow, MSG, 128), f32(narrow, MSG, 128),
+                f32(narrow, MSG, 128), f32(narrow, MSG, 128),
                 f32(wide, 9, 128), f32(wide, 9, 128),
                 f32(1, 1, 128), f32(wide, 1, 128), f32(1, 1, 128), f32(narrow, 1, 128),
                 f32(ny, 9 * 128),

time: 89 us -> 88.8 us (level)
  no operation moved by 1% of the time
where the time goes in v6:
time: 88.8 us; the launch traced here: 88.7 us
  Pallas kernels  88.7 us (100%)
    pallas_call x1, Pallas kernels, local(): pl.pallas_call(lambda *refs: fused(sizes, *refs), out_shape=(jax.ShapeDty...  86.1 us
    pallas_call x1, Pallas kernels, local(): pl.pallas_call(functools.partial(channel_mlp, sizes['count']), out_shape=...  2.63 us

profile of v6, /device:TPU:80, one launch (start us, length us, event | category | flops | bytes accessed | tf_op | source)
XLA Modules:
  0.0 88.7 jit_solution(6621951710281236084)
XLA Ops:
  0.0 86.1 %shard_map.226 = (f32[4,256,128]{2,1,0:T(8,128)S(1)}, f32[1,128]{1,0:T(1,128)S(1)}, f32[4,256,128]{2,1,0:T(8,128)S(1)}, bf16[256,256]{1,0:T(8,128)(2,1)S(1)}, bf...) custom-call(f32[1024,128]{1,0:T(8,128)} %bitcast.11, f32[32,256]{1,0:T(8,128)} %bitcast.12, ...), custom_call_target="tpu_custom_call" | custom-call | tf_op jit(solution)/shard_map/pallas_call | solution.py:558
  86.1 2.6 %shard_map.227 = f32[1024,128]{1,0:T(8,128)} custom-call(f32[4,256,128]{2,1,0:T(8,128)S(1)} %get-tuple-element.12.summed, f32[1,128]{1,0:T(1,128)S(1)} %get-tuple-element.13.stats, f32[4,256,128]{2,1,0:T(8,128)S(1)} %get-tuple-element.14.cols, bf16[256,256]{1,0:T(8,128)(2,1)S(1)} %get-tuple-element.15.in_hi, bf16[256,256]{1,0:T(8,128)(2,1)S(1)} %get-tuple-element.16.in_lo, ...), custom_call_target="tpu_custom_call" | custom-call | tf_op jit(solution)/shard_map/pallas_call | solution.py:585

commit v7 on v6

--- a/solution.py
+++ b/solution.py
@@ -274,7 +274,7 @@
     return sorted(range(1, n), key=lambda d: -min(d, n - d))
 
 
-AHEAD = 4
+AHEAD = 5
 
 
 def fused(sizes, *refs):

time: 88.8 us -> 88.6 us (level)
  no operation moved by 1% of the time
where the time goes in v7:
time: 88.6 us; the launch traced here: 88.5 us
  Pallas kernels  88.5 us (100%)
    pallas_call x1, Pallas kernels, local(): pl.pallas_call(lambda *refs: fused(sizes, *refs), out_shape=(jax.ShapeDty...  85.8 us
    pallas_call x1, Pallas kernels, local(): pl.pallas_call(functools.partial(channel_mlp, sizes['count']), out_shape=...  2.62 us

profile of v7, /device:TPU:80, one launch (start us, length us, event | category | flops | bytes accessed | tf_op | source)
XLA Modules:
  0.0 88.5 jit_solution(6953498910437108618)
XLA Ops:
  0.0 85.8 %shard_map.226 = (f32[4,256,128]{2,1,0:T(8,128)S(1)}, f32[1,128]{1,0:T(1,128)S(1)}, f32[4,256,128]{2,1,0:T(8,128)S(1)}, bf16[256,256]{1,0:T(8,128)(2,1)S(1)}, bf...) custom-call(f32[1024,128]{1,0:T(8,128)} %bitcast.11, f32[32,256]{1,0:T(8,128)} %bitcast.12, ...), custom_call_target="tpu_custom_call" | custom-call | tf_op jit(solution)/shard_map/pallas_call | solution.py:558
  85.8 2.6 %shard_map.227 = f32[1024,128]{1,0:T(8,128)} custom-call(f32[4,256,128]{2,1,0:T(8,128)S(1)} %get-tuple-element.12.summed, f32[1,128]{1,0:T(1,128)S(1)} %get-tuple-element.13.stats, f32[4,256,128]{2,1,0:T(8,128)S(1)} %get-tuple-element.14.cols, bf16[256,256]{1,0:T(8,128)(2,1)S(1)} %get-tuple-element.15.in_hi, bf16[256,256]{1,0:T(8,128)(2,1)S(1)} %get-tuple-element.16.in_lo, ...), custom_call_target="tpu_custom_call" | custom-call | tf_op jit(solution)/shard_map/pallas_call | solution.py:585
